TPU v7x, 8 devices: a whole 2x2x1 slice. The times are simulated.
8 devices in a mesh: data: 1 (over z), ys: 2 (over y), xs: 4 (over x, core).
Axes of the slice: x: 2, y: 2, z: 1, core: 2. Of those that a mesh axis runs over, the one named last changes fastest.
Arguments:
- field: float32 [8, 128, 128, 40, 20], P('data', 'xs', 'ys')
- spec_real: float32 [2, 16, 16, 8, 20, 20], replicated
- spec_imag: float32 [2, 16, 16, 8, 20, 20], replicated
- mix_weight: float32 [2, 20, 20], replicated
- bias: float32 [2, 20], replicated
Outputs:
- output: float32 [8, 128, 128, 40, 20], P('data', 'xs', 'ys')
All inputs are finite; a program needn't handle non-finite values.
Results may differ from a plain program's by a relative error of at most 0.001.
Values are sent between devices in bfloat16 or wider.
A program may use at most 1 GiB of HBM per device.

v0:
```python
import math
import jax
import jax.numpy as jnp
from jax import lax
from jax.sharding import PartitionSpec as P

EXACT_DOT = lax.Precision.HIGHEST


def kept_freqs(count, size):
    slots = jnp.arange(2 * count, dtype=jnp.int32)
    return jnp.where(slots < count, slots, slots + (size - 2 * count))


def phase_block(rows, cols, size, sign):
    angle = ((rows[:, None] * cols[None, :]) % size).astype(jnp.float32) * (2.0 * math.pi / size)
    cosine = jnp.cos(angle)
    sine = sign * jnp.sin(angle)
    return jnp.stack([jnp.stack([cosine, sine], axis=1), jnp.stack([-sine, cosine], axis=1)], axis=0)


def contract(form, left, right):
    return jnp.einsum(form, left, right, precision=EXACT_DOT, preferred_element_type=jnp.float32)


def solution(mesh):
    row_devs = mesh.shape['ys']
    col_devs = mesh.shape['xs']

    def local_layers(field, spec_real, spec_imag, mix_weight, bias):
        batch, x_loc, y_loc, grid_z, width = field.shape
        modes = spec_real.shape[3]
        grid_x = x_loc * col_devs
        grid_y = y_loc * row_devs
        yz_modes = 2 * modes * modes
        yz_local = yz_modes // row_devs
        mode_local = 2 * modes * yz_local // col_devs
        x_index = lax.axis_index('xs')
        y_index = lax.axis_index('ys')
        x_pos = x_index * x_loc + jnp.arange(x_loc, dtype=jnp.int32)
        y_pos = y_index * y_loc + jnp.arange(y_loc, dtype=jnp.int32)
        z_pos = jnp.arange(grid_z, dtype=jnp.int32)
        kx_freq = kept_freqs(modes, grid_x)
        ky_freq = kept_freqs(modes, grid_y)
        kz_freq = jnp.arange(modes, dtype=jnp.int32)
        fwd_z = phase_block(z_pos, kz_freq, grid_z, -1.0)[0]
        fwd_y = phase_block(y_pos, ky_freq, grid_y, -1.0)
        fwd_x = phase_block(x_pos, kx_freq, grid_x, -1.0)
        inv_x = phase_block(kx_freq, x_pos, grid_x, 1.0)
        inv_y = phase_block(ky_freq, y_pos, grid_y, 1.0)
        z_weight = jnp.where(kz_freq == 0, 1.0, 2.0) / (grid_x * grid_y * grid_z)
        inv_z = phase_block(kz_freq, z_pos, grid_z, 1.0)[:, :, 0, :] * z_weight[None, :, None]
        for layer in range(spec_real.shape[0]):
            along_z = contract('bxyzc,zpk->pbxykc', field, fwd_z)
            along_y = contract('pbxykc,pyqj->qbxjkc', along_z, fwd_y)
            along_y = lax.psum_scatter(along_y.reshape(2, batch, x_loc, yz_modes, width), 'ys', scatter_dimension=3, tiled=True)
            along_x = contract('pbxmc,pxqj->qbjmc', along_y, fwd_x)
            spectrum = lax.psum_scatter(along_x.reshape(2, batch, 2 * modes * yz_local, width), 'xs', scatter_dimension=2, tiled=True)
            real_w = lax.dynamic_slice_in_dim(spec_real[layer].reshape(2 * modes, yz_modes, width, width), y_index * yz_local, yz_local, axis=1)
            real_w = lax.dynamic_slice_in_dim(real_w.reshape(2 * modes * yz_local, width, width), x_index * mode_local, mode_local, axis=0)
            imag_w = lax.dynamic_slice_in_dim(spec_imag[layer].reshape(2 * modes, yz_modes, width, width), y_index * yz_local, yz_local, axis=1)
            imag_w = lax.dynamic_slice_in_dim(imag_w.reshape(2 * modes * yz_local, width, width), x_index * mode_local, mode_local, axis=0)
            real_mix = contract('pbqi,qio->pbqo', spectrum, real_w)
            imag_mix = contract('pbqi,qio->pbqo', spectrum, imag_w)
            mixed = jnp.stack([real_mix[0] - imag_mix[1], imag_mix[0] + real_mix[1]], axis=0)
            mixed = lax.all_gather(mixed, 'xs', axis=2, tiled=True).reshape(2, batch, 2 * modes, yz_local, width)
            back_x = contract('pbjmc,pjqx->qbxmc', mixed, inv_x)
            back_x = lax.all_gather(back_x, 'ys', axis=3, tiled=True).reshape(2, batch, x_loc, 2 * modes, modes, width)
            back_y = contract('pbxjkc,pjqy->qbxykc', back_x, inv_y)
            spectral = contract('pbxykc,pkz->bxyzc', back_y, inv_z)
            pointwise = jnp.dot(field, mix_weight[layer], precision=EXACT_DOT, preferred_element_type=jnp.float32)
            field = jax.nn.gelu(spectral + pointwise + bias[layer], approximate=True)
        return field

    field_spec = P('data', 'xs', 'ys', None, None)
    return jax.shard_map(local_layers, mesh=mesh, in_specs=(field_spec, P(), P(), P(), P()), out_specs=field_spec, check_vma=False)
```

profile of v0, /device:TPU:0, one launch (start us, length us, event | category | flops | bytes accessed | tf_op | source)
XLA Modules:
  0.0 2016.5 jit_solution(12138040689514174976)
XLA Ops:
  6.8 63.3 %fusion.44 = f32[2,8,32,64,8,20]{3,4,5,2,1,0:T(8,128)} fusion(f32[8,32,64,40,20]{2,3,4,1,0:T(8,128)} %param.5, f32[40,1,8]{0,2,1:T(8,128)S(1)} %get-tuple-element.39, f32[40,1,8]{0,2,1:T(8,128)S(1)} %get-tuple-element.40), kind=kOutput, calls=%fused_computation.50 | convolution fusion | flops 2516582912 | bytes 73402880 | tf_op jit(solution)/shard_map/bxyzc,zpk->pbxykc/dot_general | solution.py:23
  70.1 113.5 %fusion.54 = f32[2,8,32,16,8,20]{2,3,5,4,1,0:T(8,128)S(1)} fusion(f32[2,8,32,64,8,20]{3,4,5,2,1,0:T(8,128)} %fusion.44, f32[1,64,2,16]{1,3,0,2:T(8,128)S(1)} %get-tuple-element.22, f32[1,64,2,16]{1,3,0,2:T(8,128)S(1)} %get-tuple-element.21), kind=kOutput, calls=%fused_computation.56 | convolution fusion | flops 2013270016 | bytes 26230784 | tf_op jit(solution)/shard_map/pbxykc,pyqj->qbxjkc/dot_general | solution.py:23
  183.7 19.1 copy.172
  202.9 22.8 %fusion.161 = (f32[1,16,16,8,20,20]{5,3,4,2,1,0:T(8,128)}, f32[1,16,16,8,20,20]{5,3,4,2,1,0:T(8,128)S(1)}) fusion(f32[2,16,16,8,20,20]{5,3,4,2,1,0:T(8,128)} %param.6), kind=kLoop, calls=%fused_computation.198 | loop fusion | bytes 13107200 | tf_op jit(solution)/shard_map/slice | solution.py:59
  225.7 16.5 copy.174
  282.7 30.4 %fusion.160 = (f32[1,16,16,8,20,20]{5,3,4,2,1,0:T(8,128)}, f32[1,16,16,8,20,20]{5,3,4,2,1,0:T(8,128)}) fusion(f32[2,16,16,8,20,20]{5,3,4,2,1,0:T(8,128)} %param.7), kind=kLoop, calls=%fused_computation.197 | loop fusion | bytes 13107200 | tf_op jit(solution)/shard_map/slice | solution.py:61
  313.1 124.2 %reduce-scatter.5.cloned.1.call-done = f32[2,8,32,64,20]{2,3,4,1,0:T(8,128)} async-done(((f32[2,8,32,128,20]{2,3,4,1,0:T(8,128)}), f32[2,8,32,64,20]{2,3,4,1,0:T(8,128)}) %reduce-scatter.5.cloned.1.call-update) | async-done | bytes 2621456 | tf_op jit(solution)/shard_map/reduce_scatter | solution.py:56
  437.2 17.1 fusion.72
  459.4 29.7 %copy_bitcast_fusion = (f32[16,128,20,20]{3,1,2,0:T(8,128)}, f32[16,128,20,20]{3,1,2,0:T(8,128)}) fusion(f32[1,16,16,8,20,20]{5,3,4,2,1,0:T(8,128)} %get-tuple-element.5, f32[1,16,16,8,20,20]{5,3,4,2,1,0:T(8,128)} %get-tuple-element.6), kind=kLoop, calls=%fused_computation.42 | loop fusion | bytes 13107200 | tf_op jit(solution)/shard_map/reshape;squeeze | solution.py:61
  499.3 16.6 copy.67
  569.0 153.4 %fusion.2 = f32[8,32,64,40,20]{2,4,3,1,0:T(8,128)} fusion(f32[8,32,64,40,20]{2,3,4,1,0:T(8,128)} %param.5, f32[1,20,20]{1,2,0:T(8,128)S(1)} %copy.127), kind=kOutput, calls=%fused_computation.4 | convolution fusion | flops 3145728000 | bytes 104859200 | tf_op jit(solution)/shard_map/dot_general | solution.py:71
  723.5 90.7 %all-gather.7.cloned.1.call-done = f32[2,8,32,128,20]{2,1,4,0,3:T(8,128)} async-done(((f32[2,8,32,64,20]{2,1,4,0,3:T(8,128)}), f32[2,8,32,128,20]{2,1,4,0,3:T(8,128)}) %all-gather.7.cloned.1.call-update) | async-done | bytes 5242896 | tf_op jit(solution)/shard_map/all_gather | solution.py:68
  814.1 48.2 %fusion.38 = f32[2,8,32,64,8,20]{3,2,5,4,1,0:T(8,128)} fusion(f32[2,8,32,16,8,20]{2,1,5,0,4,3:T(8,128)} %bitcast.299, f32[1,16,2,64]{3,1,0,2:T(8,128)S(1)} %get-tuple-element.16, f32[1,16,2,64]{3,1,0,2:T(8,128)S(1)} %get-tuple-element.15), kind=kOutput, calls=%fused_computation.48 | convolution fusion | flops 2013270016 | bytes 26230784 | tf_op jit(solution)/shard_map/pbxjkc,pjqy->qbxykc/dot_general | solution.py:23
  862.3 153.9 %fusion.10 = f32[8,32,64,40,20]{2,3,4,1,0:T(8,128)} fusion(f32[8,32,64,40,20]{2,4,3,1,0:T(8,128)} %fusion.2, f32[20]{0:T(128)S(1)} %get-tuple-element.26, f32[2,8,32,64,8,20]{3,2,5,4,1,0:T(8,128)} %fusion.38, f32[2,8,40,1,1,1]{2,1,0,5,4,3:T(8,128)S(1)} %fusion.169), kind=kOutput, calls=%fused_computation.12 | convolution fusion | flops 2647654400 | bytes 125831760 | tf_op jit(solution)/shard_map/pbxykc,pkz->bxyzc/dot_general | solution.py:23
  1016.2 63.2 %fusion.47 = f32[2,8,32,64,8,20]{3,4,5,2,1,0:T(8,128)} fusion(f32[8,32,64,40,20]{2,3,4,1,0:T(8,128)} %fusion.10, f32[40,1,8]{0,2,1:T(8,128)S(1)} %copy-done.22, f32[40,1,8]{0,2,1:T(8,128)S(1)} %copy-done.24), kind=kOutput, calls=%fused_computation.51 | convolution fusion | flops 2516582912 | bytes 73402880 | tf_op jit(solution)/shard_map/bxyzc,zpk->pbxykc/dot_general | solution.py:23
  1079.4 113.3 %fusion.57 = f32[2,8,32,16,8,20]{2,3,5,4,1,0:T(8,128)S(1)} fusion(f32[2,8,32,64,8,20]{3,4,5,2,1,0:T(8,128)} %fusion.47, f32[1,64,2,16]{1,3,0,2:T(8,128)S(1)} %copy-done.3, f32[1,64,2,16]{1,3,0,2:T(8,128)S(1)} %copy-done.1), kind=kOutput, calls=%fused_computation.57 | convolution fusion | flops 2013270016 | bytes 26230784 | tf_op jit(solution)/shard_map/pbxykc,pyqj->qbxjkc/dot_general | solution.py:23
  1192.8 19.2 copy.171
  1212.0 231.5 %reduce-scatter.9.cloned.1.call-done = f32[2,8,32,64,20]{2,3,4,1,0:T(8,128)} async-done(((f32[2,8,32,128,20]{2,3,4,1,0:T(8,128)}), f32[2,8,32,64,20]{2,3,4,1,0:T(8,128)}) %reduce-scatter.9.cloned.1.call-update) | async-done | bytes 2621456 | tf_op jit(solution)/shard_map/reduce_scatter | solution.py:56
  1443.5 16.9 fusion.75
  1492.2 16.8 copy.85
  1562.3 153.5 %fusion = f32[8,32,64,40,20]{2,4,3,1,0:T(8,128)} fusion(f32[8,32,64,40,20]{2,3,4,1,0:T(8,128)} %fusion.10, f32[1,20,20]{1,2,0:T(8,128)S(1)} %copy.128), kind=kOutput, calls=%fused_computation.2 | convolution fusion | flops 3145728000 | bytes 104859200 | tf_op jit(solution)/shard_map/dot_general | solution.py:71
  1715.8 91.6 %all-gather.11.cloned.1.call-done = f32[2,8,32,128,20]{2,1,4,0,3:T(8,128)} async-done(((f32[2,8,32,64,20]{2,1,4,0,3:T(8,128)}), f32[2,8,32,128,20]{2,1,4,0,3:T(8,128)}) %all-gather.11.cloned.1.call-update) | async-done | bytes 5242896 | tf_op jit(solution)/shard_map/all_gather | solution.py:68
  1807.5 48.2 %fusion.41 = f32[2,8,32,64,8,20]{3,2,5,4,1,0:T(8,128)} fusion(f32[2,8,32,16,8,20]{2,1,5,0,4,3:T(8,128)} %bitcast.300, f32[1,16,2,64]{3,1,0,2:T(8,128)S(1)} %copy-done.15, f32[1,16,2,64]{3,1,0,2:T(8,128)S(1)} %copy-done.13), kind=kOutput, calls=%fused_computation.49 | convolution fusion | flops 2013270016 | bytes 26230784 | tf_op jit(solution)/shard_map/pbxjkc,pjqy->qbxykc/dot_general | solution.py:23
  1855.6 153.8 %fusion.17 = f32[8,32,64,40,20]{2,3,4,1,0:T(8,128)} fusion(f32[8,32,64,40,20]{2,4,3,1,0:T(8,128)} %fusion, f32[20]{0:T(128)S(1)} %copy-done.31, f32[2,8,32,64,8,20]{3,2,5,4,1,0:T(8,128)} %fusion.41, f32[2,8,40,1,1,1]{2,1,0,5,4,3:T(8,128)S(1)} %fusion.171), kind=kOutput, calls=%fused_computation.19 | convolution fusion | flops 2647654400 | bytes 125831760 | tf_op jit(solution)/shard_map/pbxykc,pkz->bxyzc/dot_general | solution.py:23
  (138 shorter events, 194.8 us)
Async XLA Ops:
  6.5 430.7 %reduce-scatter.5.cloned.1.call-start = ((), (), s32[]{:S(2)}) async-start(), calls=%async_computation.4 | async-start | bytes 31457280 | tf_op jit(solution)/shard_map/reduce_scatter | solution.py:56
  6.6 63.5 %copy-start.21 = (f32[40,1,8]{0,2,1:T(8,128)}, f32[40,1,8]{0,2,1:T(8,128)S(1)}, u32[]{:S(2)}) copy-start(f32[40,1,8]{0,2,1:T(8,128)S(1)} %get-tuple-element.39) | copy-start | bytes 3844
  202.8 313.1 %reduce-scatter.7.cloned.1.call-start = ((), (), s32[]{:S(2)}) async-start(), calls=%async_computation.5 | async-start | bytes 1638400 | tf_op jit(solution)/shard_map/reduce_scatter | solution.py:58
  282.6 154.6 %copy-start.4 = (f32[1,32,2,16]{1,3,0,2:T(8,128)}, f32[1,32,2,16]{1,3,0,2:T(8,128)S(1)}, u32[]{:S(2)}) copy-start(f32[1,32,2,16]{1,3,0,2:T(8,128)S(1)} %get-tuple-element.19) | copy-start | bytes 12292
  282.7 154.6 %copy-start.6 = (f32[1,32,2,16]{1,3,0,2:T(8,128)}, f32[1,32,2,16]{1,3,0,2:T(8,128)S(1)}, u32[]{:S(2)}) copy-start(f32[1,32,2,16]{1,3,0,2:T(8,128)S(1)} %get-tuple-element.20) | copy-start | bytes 12292
  459.3 86.6 %all-gather.5.cloned.1.call-start = ((), (), s32[]{:S(2)}) async-start(), calls=%async_computation.6 | async-start | bytes 1638400 | tf_op jit(solution)/shard_map/all_gather | solution.py:66
  530.6 283.5 %all-gather.7.cloned.1.call-start = ((), (), s32[]{:S(2)}) async-start(), calls=%async_computation.7 | async-start | bytes 31457280 | tf_op jit(solution)/shard_map/all_gather | solution.py:68
  531.5 191.0 %copy-start.8 = (f32[1,16,2,32]{3,1,0,2:T(8,128)}, f32[1,16,2,32]{3,1,0,2:T(8,128)S(1)}, u32[]{:S(2)}) copy-start(f32[1,16,2,32]{3,1,0,2:T(8,128)S(1)} %get-tuple-element.17) | copy-start | bytes 12292
  531.5 191.0 %copy-start.10 = (f32[1,16,2,32]{3,1,0,2:T(8,128)}, f32[1,16,2,32]{3,1,0,2:T(8,128)S(1)}, u32[]{:S(2)}) copy-start(f32[1,16,2,32]{3,1,0,2:T(8,128)S(1)} %get-tuple-element.18) | copy-start | bytes 12292
  569.0 153.7 %copy-start.27 = (s32[64]{0:T(128)S(1)}, s32[64]{0:T(128)}, u32[]{:S(2)}) copy-start(s32[64]{0:T(128)} %copy-done.26) | copy-start | bytes 772
  569.0 153.8 %copy-start.30 = (f32[2,20]{1,0:T(2,128)S(1)}, f32[2,20]{1,0:T(2,128)}, u32[]{:S(2)}) copy-start(f32[2,20]{1,0:T(2,128)} %param.9) | copy-start | bytes 484
  569.0 874.5 %reduce-scatter.9.cloned.1.call-start = ((), (), s32[]{:S(2)}) async-start(), calls=%async_computation.8 | async-start | bytes 31457280 | tf_op jit(solution)/shard_map/reduce_scatter | solution.py:56
  722.5 139.8 %copy-start.28 = (f32[8]{0:T(128)}, f32[8]{0:T(128)S(1)}, u32[]{:S(2)}) copy-start(f32[8]{0:T(128)S(1)} %fusion.147) | copy-start | bytes 100
  722.8 139.4 %copy-start.12 = (f32[1,16,2,64]{3,1,0,2:T(8,128)}, f32[1,16,2,64]{3,1,0,2:T(8,128)S(1)}, u32[]{:S(2)}) copy-start(f32[1,16,2,64]{3,1,0,2:T(8,128)S(1)} %get-tuple-element.15) | copy-start | bytes 24580
  722.8 139.4 %copy-start.14 = (f32[1,16,2,64]{3,1,0,2:T(8,128)}, f32[1,16,2,64]{3,1,0,2:T(8,128)S(1)}, u32[]{:S(2)}) copy-start(f32[1,16,2,64]{3,1,0,2:T(8,128)S(1)} %get-tuple-element.16) | copy-start | bytes 24580
  862.3 153.9 %copy-start.22 = (f32[40,1,8]{0,2,1:T(8,128)S(1)}, f32[40,1,8]{0,2,1:T(8,128)}, u32[]{:S(2)}) copy-start(f32[40,1,8]{0,2,1:T(8,128)} %copy-done.21) | copy-start | bytes 3844
  862.3 153.9 %copy-start.24 = (f32[40,1,8]{0,2,1:T(8,128)S(1)}, f32[40,1,8]{0,2,1:T(8,128)}, u32[]{:S(2)}) copy-start(f32[40,1,8]{0,2,1:T(8,128)} %copy-done.23) | copy-start | bytes 3844
  1212.0 231.6 %copy-start.5 = (f32[1,32,2,16]{1,3,0,2:T(8,128)S(1)}, f32[1,32,2,16]{1,3,0,2:T(8,128)}, u32[]{:S(2)}) copy-start(f32[1,32,2,16]{1,3,0,2:T(8,128)} %copy-done.4) | copy-start | bytes 12292
  1212.0 231.6 %copy-start.7 = (f32[1,32,2,16]{1,3,0,2:T(8,128)S(1)}, f32[1,32,2,16]{1,3,0,2:T(8,128)}, u32[]{:S(2)}) copy-start(f32[1,32,2,16]{1,3,0,2:T(8,128)} %copy-done.6) | copy-start | bytes 12292
  1212.0 297.1 %reduce-scatter.11.cloned.1.call-start = ((), (), s32[]{:S(2)}) async-start(), calls=%async_computation.9 | async-start | bytes 1638400 | tf_op jit(solution)/shard_map/reduce_scatter | solution.py:58
  1465.4 73.7 %all-gather.9.cloned.1.call-start = ((), (), s32[]{:S(2)}) async-start(), calls=%async_computation.10 | async-start | bytes 1638400 | tf_op jit(solution)/shard_map/all_gather | solution.py:66
  1523.8 283.7 %all-gather.11.cloned.1.call-start = ((), (), s32[]{:S(2)}) async-start(), calls=%async_computation.11 | async-start | bytes 31457280 | tf_op jit(solution)/shard_map/all_gather | solution.py:68
  1562.3 245.1 %copy-start.13 = (f32[1,16,2,64]{3,1,0,2:T(8,128)S(1)}, f32[1,16,2,64]{3,1,0,2:T(8,128)}, u32[]{:S(2)}) copy-start(f32[1,16,2,64]{3,1,0,2:T(8,128)} %copy-done.12) | copy-start | bytes 24580
  1562.3 245.1 %copy-start.15 = (f32[1,16,2,64]{3,1,0,2:T(8,128)S(1)}, f32[1,16,2,64]{3,1,0,2:T(8,128)}, u32[]{:S(2)}) copy-start(f32[1,16,2,64]{3,1,0,2:T(8,128)} %copy-done.14) | copy-start | bytes 24580
  (16 other events, 659.9 us)
Sparse Core Ops, SparseCore 0:
  203.0 234.2 reduce-scatter.4
  459.4 20.7 reduce-scatter.6
  530.7 15.1 all-gather.4
  569.1 244.9 all-gather.6
  1212.1 231.3 reduce-scatter.8
  1465.5 20.7 reduce-scatter.10
  1523.9 15.1 all-gather.8
  1562.4 244.9 all-gather.10
where the time goes:
time: 2020 us
  matrix products  1130 us (56%)
  waiting for transfers between devices  568 us (28%)
  local copies, waits for them, and re-layouts  300 us (15%)
    dot_general x12, matrix products, contract(): jnp.einsum(form, left, right, precision=EXACT_DOT, preferred_element_type...  804 us
    reduce_scatter x2, waiting for transfers between devices, local_layers(): lax.psum_scatter(along_y.reshape(2, batch, x_loc, yz_modes, width), 'ys',...  356 us
    dot_general x2, matrix products, local_layers(): jnp.dot(field, mix_weight[layer], precision=EXACT_DOT, preferred_element_...  307 us
    all_gather x2, waiting for transfers between devices, local_layers(): lax.all_gather(back_x, 'ys', axis=3, tiled=True)  182 us
    transpose x4, local copies, waits for them, and re-layouts, contract(): jnp.einsum(form, left, right, precision=EXACT_DOT, preferred_element_type...  60.5 us
    dynamic_slice x4, local copies, waits for them, and re-layouts, local_layers(): lax.dynamic_slice_in_dim(spec_imag[layer].reshape(2 * modes, yz_modes, wi...  53.7 us
    dynamic_slice x3, local copies, waits for them, and re-layouts, local_layers(): lax.dynamic_slice_in_dim(spec_real[layer].reshape(2 * modes, yz_modes, wi...  48.9 us
    slice x3, local copies, waits for them, and re-layouts, local_layers(): spec_real[layer].reshape(2 * modes, yz_modes, width, width)  47.1 us
  transfers between devices with their start and end apart: 8, of which 6 were waited for; matrix products, arithmetic and copies ran while one was open for 26% of the time, Pallas kernels for 0%

commit v1 on v0

v1 whole, which is shorter than its diff:
```python
import functools
import math

import jax
import jax.numpy as jnp
import numpy as np
from jax import lax
from jax.experimental import pallas as pl
from jax.experimental.pallas import tpu as pltpu
from jax.sharding import PartitionSpec as P

F32 = jnp.float32
BF16 = jnp.bfloat16
LANES = 256
CHUNKS = 2
PACK = 384


def split_xla(v):
    hi = lax.reduce_precision(v, 8, 7)
    rest = v - hi
    mid = lax.reduce_precision(rest, 8, 7)
    return hi.astype(BF16), mid.astype(BF16), (rest - mid).astype(BF16)


def split_np(v):
    v = np.asarray(v, np.float32)
    hi = v.astype(BF16)
    rest = v - hi.astype(np.float32)
    mid = rest.astype(BF16)
    return hi, mid, (rest - mid.astype(np.float32)).astype(BF16)


def split3(v):
    hi = v.astype(BF16)
    rest = v - hi.astype(F32)
    mid = rest.astype(BF16)
    return hi, mid, (rest - mid.astype(F32)).astype(BF16)


def dot(a, b):
    return jnp.dot(a, b, preferred_element_type=F32)


def dot6(a, b):
    return (dot(a[2], b[0]) + dot(a[1], b[1]) + dot(a[0], b[2])) + (dot(a[1], b[0]) + dot(a[0], b[1])) + dot(a[0], b[0])


def six_rows(s):
    return jnp.concatenate([s[0], s[0], s[0], s[1], s[1], s[2]], axis=0)


def six_cols(s, xp=jnp):
    return xp.concatenate([s[0], s[1], s[2], s[0], s[1], s[0]], axis=1)


def lane_map(modes):
    lanes = {}
    for k in range(modes):
        for j in range(2 * modes):
            lanes[k, j] = k * 2 * modes + j
    for k in range(modes):
        lanes[k, 2 * modes] = 128 + k
    for j in range(2 * modes + 1):
        lanes[modes, j] = 128 + modes + j
    return lanes


def tables(modes, grid_x, grid_y, grid_z, x_loc, y_loc, col_devs, row_devs):
    lanes = lane_map(modes)
    used = np.zeros(LANES)
    k_of = np.zeros(LANES)
    j_of = np.zeros(LANES, np.int64)
    for (k, j), lane in lanes.items():
        used[lane], k_of[lane], j_of[lane] = 1.0, k, j
    u = np.arange(x_loc // 2) - (x_loc - 1) / 2.0
    ang = 2 * np.pi * u[:, None] * k_of[None, :] / grid_x
    cos_u, sin_u = np.cos(ang) * used, np.sin(ang) * used
    centre = np.arange(col_devs) * x_loc + (x_loc - 1) / 2.0
    ang = 2 * np.pi * centre[:, None] * k_of[None, :] / grid_x
    p, q = np.cos(ang) * used, np.sin(ang) * used
    y = np.arange(grid_y)
    freq = np.where(j_of <= modes, j_of, j_of - modes)
    ang = 2 * np.pi * ((y[:, None] * freq[None, :]) % grid_y) / grid_y
    trig_y = (np.where(j_of <= modes, np.cos(ang), np.sin(ang)) * used).reshape(row_devs, y_loc, LANES)
    z = np.arange(grid_z)
    kz = np.arange(modes)
    ang = 2 * np.pi * ((z[:, None] * kz[None, :]) % grid_z) / grid_z
    trig_z = np.concatenate([np.cos(ang), np.sin(ang)], axis=1)
    weight = np.where(kz == 0, 1.0, 2.0) / (grid_x * grid_y * grid_z)
    inv_z = trig_z * np.concatenate([weight, weight])[None, :]
    fwd2 = split_np(np.kron(np.eye(2), trig_z.T))
    zero = np.zeros_like(fwd2[0])
    z_fwd = np.concatenate([
        np.concatenate([fwd2[0], fwd2[0], fwd2[0]], axis=1),
        np.concatenate([fwd2[1], fwd2[1], zero], axis=1),
        np.concatenate([fwd2[2], zero, zero], axis=1)], axis=0)
    z_inv = six_cols(split_np(np.kron(np.eye(2), inv_z)), np)
    count = 2 * modes
    sign = np.zeros((2 * count * count, PACK), np.float32)
    where_a = lambda lane: lane if lane < 128 else 128 + lane
    where_b = lambda lane: 128 + lane if lane < 128 else 192 + lane
    for ix in range(count):
        sx, kx = (1, ix) if ix < modes else (-1, count - ix)
        for iy in range(count):
            sy, ky = (1, iy) if iy < modes else (-1, count - iy)
            re = ix * count + iy
            im = re + count * count
            sign[re, where_a(lanes[kx, ky])] += 1
            if kx and ky:
                sign[re, where_b(lanes[kx, modes + ky])] -= sx * sy
            if kx:
                sign[im, where_b(lanes[kx, ky])] -= sx
            if ky:
                sign[im, where_a(lanes[kx, modes + ky])] -= sy
    f32 = lambda a: np.asarray(a, np.float32)
    return dict(cos_u=f32(cos_u), sin_u=f32(sin_u), pq=f32(np.stack([p, q], axis=1)), trig_y=f32(trig_y),
                z_fwd=z_fwd, z_inv=z_inv, to_trig=sign.astype(BF16), to_modes=sign.T.astype(BF16))


def forward_rows(v, z_fwd_ref, zs_ref, side, pair):
    y = dot(z_fwd_ref[...], jnp.concatenate(split3(v), axis=0))
    rows = y.shape[0] // 3
    zs_ref[side, pair * rows:(pair + 1) * rows, :] = y[:rows] + (y[rows:2 * rows] + y[2 * rows:])


def forward_xy(g, zs_ref, xy_ref, acc_ref):
    plus, minus = zs_ref[0], zs_ref[1]
    for part, v in enumerate((plus + minus, plus - minus)):
        new = dot6(split3(v), [xy_ref[part, t, g] for t in range(3)])

        @pl.when(g == 0)
        def _():
            acc_ref[part] = new

        @pl.when(g > 0)
        def _():
            acc_ref[part] += new


def forward_flush(acc_ref, pq_ref, rows_ref, out_ref, width, trigs):
    p, q = pq_ref[0:1], pq_ref[1:2]
    even, odd = acc_ref[0], acc_ref[1]
    a = p * even - q * odd
    b = q * even + p * odd
    tail = a[:, 128:] + pltpu.roll(b[:, 128:], 64, 1)
    packed = jnp.concatenate([a[:, :128], b[:, :128], tail], axis=1)
    rows_ref[...] = packed.reshape(width, trigs, PACK)
    half = trigs // 2
    for t in range(trigs):
        out_ref[t % half, 0, (t // half) * width:(t // half + 1) * width, :] = rows_ref[:, t, :]


def forward_kernel(width, trigs, p_ref, q_ref, z_fwd_ref, xy_ref, pq_ref, out_ref, zs_ref, acc_ref, rows_ref):
    g = pl.program_id(1)
    count = p_ref.shape[1]
    for side, ref in enumerate((p_ref, q_ref)):
        order = range(count) if side == 0 else range(count - 1, -1, -1)
        for pair in range(width // 2):
            v = jnp.concatenate([ref[0, i, 2 * pair:2 * pair + 2].reshape(-1, ref.shape[4]) for i in order], axis=1)
            forward_rows(v, z_fwd_ref, zs_ref, side, pair)
    forward_xy(g, zs_ref, xy_ref, acc_ref)

    @pl.when(g == pl.num_programs(1) - 1)
    def _():
        forward_flush(acc_ref, pq_ref, rows_ref, out_ref, width, trigs)


def inverse_xy(g, coef_ref, pq_ref, rows_ref, gs_ref, xyt_ref, sp_ref, width, trigs):
    @pl.when(g == 0)
    def _():
        half = trigs // 2
        for t in range(trigs):
            rows_ref[:, t, :] = coef_ref[t % half, 0, (t // half) * width:(t // half + 1) * width, :]
        packed = rows_ref[...].reshape(width * trigs, PACK)
        p, q = pq_ref[0:1], pq_ref[1:2]
        tail = packed[:, 256:]
        a = jnp.concatenate([packed[:, :128], tail], axis=1)
        b = jnp.concatenate([packed[:, 128:256], pltpu.roll(tail, 64, 1)], axis=1)
        for part, v in enumerate((p * a + q * b, p * b - q * a)):
            for t, s in enumerate(split3(v)):
                gs_ref[part, t] = s

    even, odd = [dot6([gs_ref[part, t] for t in range(3)], [xyt_ref[part, t, g] for t in range(3)]) for part in range(2)]
    for side, v in enumerate((even + odd, even - odd)):
        for t, s in enumerate(split3(v)):
            sp_ref[side, t] = s


def layer_side(side, load, mix_ref, z_inv_ref, bias_ref, sp_ref, u_ref, width, trigs, grid_z, emit):
    for tile in range(grid_z // 8):
        v = load(tile)
        y = dot(mix_ref[...], six_rows(split3(v)))
        u_ref[:, tile * 8:(tile + 1) * 8, :] = y.reshape(width, 8, LANES)
    for pair in range(width // 2):
        rows = slice(pair * 2 * trigs, (pair + 1) * 2 * trigs)
        y = dot(z_inv_ref[...], six_rows([sp_ref[side, t, rows, :] for t in range(3)]))
        size = 2 * grid_z
        bias = bias_ref[pair * size:(pair + 1) * size, :]
        h = y + (u_ref[2 * pair:2 * pair + 2].reshape(size, LANES) + jnp.concatenate([bias, bias], axis=1))
        emit(pair, jax.nn.gelu(h, approximate=True))


def middle_kernel(width, trigs, grid_z, p_ref, q_ref, coef_ref, mix_ref, z_inv_ref, bias_ref, z_fwd_ref, xy_ref, xyt_ref, pq_ref,
                  v_ref, out_ref, rows_ref, gs_ref, sp_ref, u_ref, zs_ref, acc_ref):
    g = pl.program_id(1)
    count = p_ref.shape[1]
    inverse_xy(g, coef_ref, pq_ref, rows_ref, gs_ref, xyt_ref, sp_ref, width, trigs)
    for side, ref in enumerate((p_ref, q_ref)):
        order = range(count) if side == 0 else range(count - 1, -1, -1)

        def load(tile):
            return jnp.concatenate([ref[0, i, :, tile * 8:(tile + 1) * 8, :].reshape(8 * width, -1) for i in order], axis=1)

        def emit(pair, v):
            size = 2 * grid_z
            v_ref[0, 0, side, pair * size:(pair + 1) * size, :] = v
            forward_rows(v, z_fwd_ref, zs_ref, side, pair)

        layer_side(side, load, mix_ref, z_inv_ref, bias_ref, sp_ref, u_ref, width, trigs, grid_z, emit)
    forward_xy(g, zs_ref, xy_ref, acc_ref)

    @pl.when(g == pl.num_programs(1) - 1)
    def _():
        forward_flush(acc_ref, pq_ref, rows_ref, out_ref, width, trigs)


def last_kernel(width, trigs, grid_z, v_ref, coef_ref, mix_ref, z_inv_ref, bias_ref, xyt_ref, pq_ref,
                out_ref, rows_ref, gs_ref, sp_ref, u_ref):
    g = pl.program_id(1)
    y_loc = out_ref.shape[4]
    count = LANES // y_loc
    inverse_xy(g, coef_ref, pq_ref, rows_ref, gs_ref, xyt_ref, sp_ref, width, trigs)
    for side in range(2):
        def load(tile):
            v = v_ref[0, 0, side].reshape(width, grid_z, LANES)[:, tile * 8:(tile + 1) * 8, :]
            return v.reshape(width * 8, LANES)

        def emit(pair, v):
            for i in range(count):
                x = count * g + i if side == 0 else out_ref.shape[1] - 1 - count * g - i
                out_ref[0, x, 2 * pair:2 * pair + 2] = v[:, i * y_loc:(i + 1) * y_loc].reshape(2, grid_z, y_loc)

        layer_side(side, load, mix_ref, z_inv_ref, bias_ref, sp_ref, u_ref, width, trigs, grid_z, emit)


def mix_kernel(width, in_ref, re_ref, im_ref, to_modes_ref, to_trig_ref, out_ref, f_ref, t_ref):
    batch, rows, _ = in_ref.shape
    n = re_ref.shape[2]
    f_ref[...] = sum(dot(s, to_modes_ref[...]) for s in split3(in_ref[...].reshape(batch * rows, PACK))[::-1]).reshape(batch, rows, 2 * n)

    def one(b, carry):
        f_cos, f_sin = f_ref[b, :width, :], f_ref[b, width:, :]
        s_re = f_cos[:, :n] + f_sin[:, n:]
        s_im = f_cos[:, n:] - f_sin[:, :n]
        t_re = jnp.zeros((width, n), F32)
        t_im = jnp.zeros((width, n), F32)
        for c in range(width):
            w_re, w_im = re_ref[c], im_ref[c]
            a, d = s_re[c:c + 1], s_im[c:c + 1]
            t_re += a * w_re - d * w_im
            t_im += a * w_im + d * w_re
        t_ref[b, :width, :] = jnp.concatenate([t_re, t_im], axis=1)
        t_ref[b, width:, :] = jnp.concatenate([-t_im, t_re], axis=1)
        return carry

    lax.fori_loop(0, batch, one, 0)
    out = sum(dot(s, to_trig_ref[...]) for s in split3(t_ref[...].reshape(batch * rows, 2 * n))[::-1])
    out_ref[...] = out.reshape(batch, rows, PACK)


def full(shape):
    return pl.BlockSpec(shape, lambda *_: (0,) * len(shape))


def params(mib, grid=2):
    return pltpu.CompilerParams(dimension_semantics=('arbitrary',) * grid, vmem_limit_bytes=mib * 2 ** 20)


def solution(mesh):
    row_devs = mesh.shape['ys']
    col_devs = mesh.shape['xs']

    def local_layers(field, spec_real, spec_imag, mix_weight, bias):
        batch, x_loc, y_loc, grid_z, width = field.shape
        layers = spec_real.shape[0]
        modes = spec_real.shape[3]
        trigs = 2 * modes
        rows = width * trigs
        count = LANES // y_loc
        groups = x_loc // (2 * count)
        t = tables(modes, x_loc * col_devs, y_loc * row_devs, grid_z, x_loc, y_loc, col_devs, row_devs)
        x_index = lax.axis_index('xs')
        y_index = lax.axis_index('ys')
        trig_y = lax.dynamic_index_in_dim(jnp.asarray(t['trig_y']), y_index, 0, keepdims=False)
        pq = lax.dynamic_index_in_dim(jnp.asarray(t['pq']), x_index, 0, keepdims=False)
        trig_x = jnp.stack([jnp.asarray(t['cos_u']), jnp.asarray(t['sin_u'])])
        xy = (trig_x[:, :, None, :] * trig_y[None, None]).reshape(2, groups, LANES, LANES)
        xy = jnp.stack(split_xla(xy), axis=1)
        xyt = jnp.swapaxes(xy, 3, 4)
        z_fwd, z_inv = jnp.asarray(t['z_fwd']), jnp.asarray(t['z_inv'])
        to_modes, to_trig = jnp.asarray(t['to_modes']), jnp.asarray(t['to_trig'])
        eye = jnp.eye(8, dtype=F32)
        mix = [six_cols(split_xla(jnp.einsum('cd,zw->dzcw', mix_weight[l], eye, precision=lax.Precision.HIGHEST).reshape(8 * width, 8 * width))) for l in range(layers)]
        bias_rows = jnp.broadcast_to(bias[:, :, None, None], (layers, width, grid_z, 128)).reshape(layers, width * grid_z, 128)
        kz = y_index * col_devs + x_index

        def own(w):
            w = lax.dynamic_index_in_dim(w, kz, 3, keepdims=False)
            return jnp.transpose(w, (0, 3, 4, 1, 2)).reshape(layers, width, width, trigs * trigs)

        real_w, imag_w = own(spec_real), own(spec_imag)

        native = jnp.transpose(field, (0, 1, 4, 3, 2))
        chunk = batch // CHUNKS
        xy_spec = full(xy.shape)
        spectrum = jax.ShapeDtypeStruct((modes, chunk, 2 * width, PACK), F32)
        spec_block = pl.BlockSpec((modes, 1, 2 * width, PACK), lambda b, g: (0, b, 0, 0))
        packed = jax.ShapeDtypeStruct((chunk, groups, 2, width * grid_z, LANES), F32)
        packed_block = pl.BlockSpec((1, 1, 2, width * grid_z, LANES), lambda b, g: (b, g, 0, 0, 0))
        rows_scr = pltpu.VMEM((width, trigs, PACK), F32)
        zs_scr = pltpu.VMEM((2, rows, LANES), F32)
        acc_scr = pltpu.VMEM((2, rows, LANES), F32)
        gs_scr = pltpu.VMEM((2, 3, rows, LANES), BF16)
        sp_scr = pltpu.VMEM((2, 3, rows, LANES), BF16)
        u_scr = pltpu.VMEM((width, grid_z, LANES), F32)

        def field_blocks(first):
            shape = (1, count, width, grid_z, y_loc)
            return [pl.BlockSpec(shape, lambda b, g: (first + b, g, 0, 0, 0)),
                    pl.BlockSpec(shape, lambda b, g: (first + b, 2 * groups - 1 - g, 0, 0, 0))]

        def cost(us):
            return pl.CostEstimate(flops=int(us * chunk * 4e7), bytes_accessed=chunk * 13 * 2 ** 20, transcendentals=0)

        def forward(first):
            return pl.pallas_call(
                functools.partial(forward_kernel, width, trigs), grid=(chunk, groups),
                in_specs=field_blocks(first) + [full(z_fwd.shape), xy_spec, full(pq.shape)],
                out_specs=spec_block, out_shape=spectrum, scratch_shapes=[zs_scr, acc_scr, rows_scr],
                compiler_params=params(56), cost_estimate=cost(8), name='forward')(native, native, z_fwd, xy, pq)

        def middle(first, coef):
            return pl.pallas_call(
                functools.partial(middle_kernel, width, trigs, grid_z), grid=(chunk, groups),
                in_specs=field_blocks(first) + [spec_block, full(mix[0].shape), full(z_inv.shape), full(bias_rows.shape[1:]), full(z_fwd.shape), xy_spec, xy_spec, full(pq.shape)],
                out_specs=[packed_block, spec_block], out_shape=[packed, spectrum],
                scratch_shapes=[rows_scr, gs_scr, sp_scr, u_scr, zs_scr, acc_scr],
                compiler_params=params(60), cost_estimate=cost(22), name='middle')(
                    native, native, coef, mix[0], z_inv, bias_rows[0], z_fwd, xy, xyt, pq)

        def last(first, v, coef, out):
            specs = [packed_block, spec_block, full(mix[1].shape), full(z_inv.shape), full(bias_rows.shape[1:]), xy_spec, full(pq.shape)]
            args = [v, coef, mix[1], z_inv, bias_rows[1], xyt, pq]
            kernel = functools.partial(last_kernel, width, trigs, grid_z)
            if out is not None:
                specs, args = [pl.BlockSpec(memory_space=pl.ANY)] + specs, [out] + args
            body = kernel if out is None else lambda unused, *refs: kernel(*refs)
            return pl.pallas_call(
                body, grid=(chunk, groups), in_specs=specs,
                out_specs=pl.BlockSpec((1, x_loc, width, grid_z, y_loc), lambda b, g: (first + b, 0, 0, 0, 0)),
                out_shape=jax.ShapeDtypeStruct(native.shape, F32), scratch_shapes=[rows_scr, gs_scr, sp_scr, u_scr],
                input_output_aliases={} if out is None else {0: 0},
                compiler_params=params(60), cost_estimate=cost(12), name='last')(*args)

        mixing = pl.pallas_call(
            functools.partial(mix_kernel, width), out_shape=jax.ShapeDtypeStruct((chunk, 2 * width, PACK), F32),
            scratch_shapes=[pltpu.VMEM((chunk, 2 * width, 2 * trigs * trigs), F32)] * 2, cost_estimate=cost(0.3),
            compiler_params=pltpu.CompilerParams(vmem_limit_bytes=32 * 2 ** 20), name='mixing')

        def gather_sum(partial):
            return lax.psum_scatter(partial, ('ys', 'xs'), scatter_dimension=0, tiled=False)

        def spread(own_sum, layer):
            mixed = mixing(own_sum, real_w[layer], imag_w[layer], to_modes, to_trig)
            return lax.all_gather(mixed, ('ys', 'xs'), axis=0, tiled=False)

        parts = [gather_sum(forward(i * chunk)) for i in range(CHUNKS)]
        coefs = [spread(part, 0) for part in parts]
        done = [middle(i * chunk, coef) for i, coef in enumerate(coefs)]
        parts = [gather_sum(partial) for v, partial in done]
        coefs = [spread(part, 1) for part in parts]
        out = None
        for i in range(CHUNKS):
            out = last(i * chunk, done[i][0], coefs[i], out)
        return jnp.transpose(out, (0, 1, 4, 3, 2))

    field_spec = P('data', 'xs', 'ys', None, None)
    return jax.shard_map(local_layers, mesh=mesh, in_specs=(field_spec, P(), P(), P(), P()), out_specs=field_spec, check_vma=False)
```

time: 2020 us -> 531 us (0.26)
  matrix products: 1130 us -> 0 us
  waiting for transfers between devices: 568 us -> 47.7 us
  Pallas kernels: 0 us -> 374 us
  local copies, waits for them, and re-layouts: 300 us -> 85.1 us
    dot_general x14 -> x0, matrix products: 1110 us -> none  [the longest x12 804 us: contract(): jnp.einsum(form, left, right, precision=EXACT_DOT, preferred_element_type...]
    pallas_call x0 -> x10, Pallas kernels: none -> 374 us  [the longest x2 186 us: middle(): pl.pallas_call(functools.partial(middle_kernel, width, trigs, grid_z), gr...]
    reduce_scatter x4, waiting for transfers between devices: 356 us -> 13.8 us  [gather_sum(): lax.psum_scatter(partial, ('ys', 'xs'), scatter_dimension=0, tiled=False)]
    all_gather x4, waiting for transfers between devices: 212 us -> 33.8 us  [spread(): return lax.all_gather(mixed, ('ys', 'xs'), axis=0, tiled=False)]
    dynamic_slice x7 -> x1, local copies, waits for them, and re-layouts: 103 us -> 29 us  [own(): w = lax.dynamic_index_in_dim(w, kz, 3, keepdims=False)]
    transpose x4 -> x0, local copies, waits for them, and re-layouts: 60.5 us -> none  [contract(): jnp.einsum(form, left, right, precision=EXACT_DOT, preferred_element_type...]
    slice x5 -> x8, local copies, waits for them, and re-layouts: 78.1 us -> 21.3 us  [the longest x6 21.3 us: spread(): mixed = mixing(own_sum, real_w[layer], imag_w[layer], to_modes, to_trig)]
    another operation x1, local copies, waits for them, and re-layouts: 29.7 us -> 2.82 us  [local_layers(): xy = jnp.stack(split_xla(xy), axis=1)]
  transfers between devices with their start and end apart: 8 -> 8, of which waited for: 6 -> 3; matrix products, arithmetic and copies ran while one was open for 26% -> 14% of each run, Pallas kernels for 0% -> 54%
where the time goes in v1:
time: 531 us; the launch traced here: 526 us
  Pallas kernels  374 us (70%)
  local copies, waits for them, and re-layouts  85.1 us (16%)
  waiting for transfers between devices  47.7 us (9%)
  between operations  14 us (3%)
    pallas_call x2, Pallas kernels, middle(): pl.pallas_call(functools.partial(middle_kernel, width, trigs, grid_z), gr...  186 us
    pallas_call x2, Pallas kernels, last(): pl.pallas_call(body, grid=(chunk, groups), in_specs=specs, out_specs=pl.B...  106 us
    pallas_call x2, Pallas kernels, forward(): pl.pallas_call(functools.partial(forward_kernel, width, trigs), grid=(chu...  72.8 us
    all_gather x4, waiting for transfers between devices, spread(): return lax.all_gather(mixed, ('ys', 'xs'), axis=0, tiled=False)  33.8 us
    dynamic_slice x1, local copies, waits for them, and re-layouts, own(): w = lax.dynamic_index_in_dim(w, kz, 3, keepdims=False)  29 us
    slice x6, local copies, waits for them, and re-layouts, spread(): mixed = mixing(own_sum, real_w[layer], imag_w[layer], to_modes, to_trig)  21.3 us
    reduce_scatter x4, waiting for transfers between devices, gather_sum(): lax.psum_scatter(partial, ('ys', 'xs'), scatter_dimension=0, tiled=False)  13.8 us
    squeeze x4, local copies, waits for them, and re-layouts, spread(): mixed = mixing(own_sum, real_w[layer], imag_w[layer], to_modes, to_trig)  11.8 us
  transfers between devices with their start and end apart: 8, of which 3 were waited for; matrix products, arithmetic and copies ran while one was open for 14% of the time, Pallas kernels for 54%

profile of v1, /device:TPU:0, one launch (start us, length us, event | category | flops | bytes accessed | tf_op | source)
XLA Modules:
  0.0 526.0 jit_solution(4845207261168595798)
XLA Ops:
  13.8 2.8 copy.39.xy_ref
  17.9 36.4 %forward.2 = f32[8,4,40,384]{3,2,1,0:T(8,128)} custom-call(f32[8,32,20,40,64]{4,3,2,1,0:T(8,128)} %bitcast.p_ref.q_ref, f32[8,32,20,40,64]{4,3,2,1,0:T(8,128)} %bitcast.p_ref.q_ref, bf16[96,240]{1,0:T(8,128)(2,1)} %constant.48.clone.z_fwd_ref, bf16[2,3,4,256,256]{4,3,2,1,0:T(8,128)(2,1)} %copy.39.xy_ref, f32[2,256]{1,0:T(2,128)} %dynamic-slice_bitcast_fusion.1.pq_ref.refs_6_), custom_call_target="tpu_custom_call" | custom-call | flops 1280000000 | bytes 54525952 | tf_op jit(solution)/shard_map/forward/pallas_call | solution.py:337
  54.3 36.5 %forward.3 = f32[8,4,40,384]{3,2,1,0:T(8,128)} custom-call(f32[8,32,20,40,64]{4,3,2,1,0:T(8,128)} %bitcast.p_ref.q_ref, f32[8,32,20,40,64]{4,3,2,1,0:T(8,128)} %bitcast.p_ref.q_ref, bf16[96,240]{1,0:T(8,128)(2,1)} %constant.48.clone.z_fwd_ref, bf16[2,3,4,256,256]{4,3,2,1,0:T(8,128)(2,1)} %copy.39.xy_ref, f32[2,256]{1,0:T(2,128)} %dynamic-slice_bitcast_fusion.1.pq_ref.refs_6_), custom_call_target="tpu_custom_call" | custom-call | flops 1280000000 | bytes 54525952 | tf_op jit(solution)/shard_map/forward/pallas_call | solution.py:337
  91.2 29.0 %constant_dynamic-slice_fusion = (f32[2,16,16,1,20,20]{5,3,4,2,1,0:T(1,128)S(1)}, f32[2,16,16,1,20,20]{5,3,4,2,1,0:T(1,128)}) fusion(f32[2,16,16,8,20,20]{5,3,4,2,1,0:T(8,128)} %param.15, s32[]{:T(128)S(6)} %select_n.15, f32[2,16,16,8,20,20]{5,3,4,2,1,0:T(8,128)} %param.14), kind=kLoop, calls=%fused_computation.24 | loop fusion | bytes 3276804 | tf_op jit(solution)/shard_map/jit(dynamic_index_in_dim)/dynamic_slice | solution.py:309
  122.6 3.6 copy.43
  126.2 2.9 squeeze.43.im_ref
  129.2 3.0 copy.62
  132.2 2.6 fusion.6
  134.8 4.8 copy.41
  139.6 3.0 squeeze.41.re_ref
  143.6 2.3 mixing.4
  153.3 17.0 %all-gather.9.cloned.1.call-done = f32[32,40,384]{2,1,0:T(8,128)} async-done(((f32[4,40,384]{2,1,0:T(8,128)}), f32[32,40,384]{2,1,0:T(8,128)}) %all-gather.9.cloned.1.call-update) | async-done | bytes 1966096 | tf_op jit(solution)/shard_map/all_gather | solution.py:376
  171.2 92.8 %middle.2 = (f32[4,4,2,800,256]{4,3,2,1,0:T(8,128)}, f32[8,4,40,384]{3,2,1,0:T(8,128)}) custom-call(f32[8,32,20,40,64]{4,3,2,1,0:T(8,128)} %bitcast.p_ref.q_ref, f32[8,32,20,40,64]{4,3,2,1,0:T(8,128)} %bitcast.p_ref.q_ref, f32[8,4,40,384]{3,2,1,0:T(8,128)} %bitcast.58, bf16[160,960]{1,0:T(8,128)(2,1)} %concatenate.6.mix_ref, ...), custom_call_target="tpu_custom_call" | custom-call | flops 3520000000 | bytes 54525952 | tf_op jit(solution)/shard_map/middle/pallas_call | solution.py:344
  264.1 93.0 %middle.3 = (f32[4,4,2,800,256]{4,3,2,1,0:T(8,128)}, f32[8,4,40,384]{3,2,1,0:T(8,128)}) custom-call(f32[8,32,20,40,64]{4,3,2,1,0:T(8,128)} %bitcast.p_ref.q_ref, f32[8,32,20,40,64]{4,3,2,1,0:T(8,128)} %bitcast.p_ref.q_ref, f32[8,4,40,384]{3,2,1,0:T(8,128)} %bitcast.57, bf16[160,960]{1,0:T(8,128)(2,1)} %concatenate.6.mix_ref, ...), custom_call_target="tpu_custom_call" | custom-call | flops 3520000000 | bytes 54525952 | tf_op jit(solution)/shard_map/middle/pallas_call | solution.py:344
  357.4 3.6 copy.48
  361.0 2.9 squeeze.46.im_ref
  363.9 4.8 copy.47
  368.7 2.9 squeeze.45.re_ref
  372.6 2.3 mixing.5
  375.2 13.7 %reduce-scatter.11.cloned.1.call-done = f32[1,4,40,384]{3,2,1,0:T(8,128)} async-done(((f32[8,4,40,384]{3,2,1,0:T(8,128)}), f32[1,4,40,384]{3,2,1,0:T(8,128)}) %reduce-scatter.11.cloned.1.call-update) | async-done | bytes 245776 | tf_op jit(solution)/shard_map/reduce_scatter | solution.py:372
  389.8 2.3 mixing.7
  395.4 16.8 %all-gather.11.cloned.1.call-done = f32[32,40,384]{2,1,0:T(8,128)} async-done(((f32[4,40,384]{2,1,0:T(8,128)}), f32[32,40,384]{2,1,0:T(8,128)}) %all-gather.11.cloned.1.call-update) | async-done | bytes 1966096 | tf_op jit(solution)/shard_map/all_gather | solution.py:376
  413.1 52.9 %last.2.unused = f32[8,32,20,40,64]{4,3,2,1,0:T(8,128)} custom-call(f32[4,4,2,800,256]{4,3,2,1,0:T(8,128)} %get-tuple-element.9.v_ref, f32[8,4,40,384]{3,2,1,0:T(8,128)} %bitcast.59, bf16[160,960]{1,0:T(8,128)(2,1)} %concatenate.7.mix_ref.refs_2_, bf16[80,192]{1,0:T(8,128)(2,1)} %constant.49.clone.z_inv_ref.refs_3_, ...), custom_call_target="tpu_custom_call" | custom-call | flops 1920000000 | bytes 54525952 | tf_op jit(solution)/shard_map/last/pallas_call | solution.py:359
  466.0 53.0 %last.3 = f32[8,32,20,40,64]{4,3,2,1,0:T(8,128)} custom-call(f32[8,32,20,40,64]{4,3,2,1,0:T(8,128)} %last.2.unused, f32[4,4,2,800,256]{4,3,2,1,0:T(8,128)} %get-tuple-element.11.refs_0_, f32[8,4,40,384]{3,2,1,0:T(8,128)} %bitcast.56, bf16[160,960]{1,0:T(8,128)(2,1)} %concatenate.7.mix_ref.refs_2_, ...), custom_call_target="tpu_custom_call", output_to_operand_aliasing={{}: (0, {})} | custom-call | flops 1920000000 | bytes 54525952 | tf_op jit(solution)/shard_map/last/pallas_call | solution.py:359
  (70 shorter events, 27.1 us)
Async XLA Ops:
  6.5 1.3 copy-start.7
  6.5 136.1 %reduce-scatter.5.cloned.1.call-start = ((), (), s32[]{:S(2)}) async-start(), calls=%async_computation.4 | async-start | bytes 2211840 | tf_op jit(solution)/shard_map/reduce_scatter | solution.py:372
  54.3 91.7 %reduce-scatter.9.cloned.1.call-start = ((), (), s32[]{:S(2)}) async-start(), calls=%async_computation.6 | async-start | bytes 2211840 | tf_op jit(solution)/shard_map/reduce_scatter | solution.py:372
  90.8 79.5 %all-gather.9.cloned.1.call-start = ((), (), s32[]{:S(2)}) async-start(), calls=%async_computation.8 | async-start | bytes 2211840 | tf_op jit(solution)/shard_map/all_gather | solution.py:376
  139.6 3.1 copy-start
  139.6 3.1 copy-start.1
  139.6 10.4 %copy-start.8 = (f32[2,20,20]{2,0,1:T(2,128)S(1)}, f32[2,20,20]{2,0,1:T(2,128)}, u32[]{:S(2)}) copy-start(f32[2,20,20]{2,0,1:T(2,128)} %param.16) | copy-start | bytes 9604
  142.6 7.2 %copy-start.9 = (f32[2,20]{1,0:T(2,128)S(1)}, f32[2,20]{1,0:T(2,128)}, u32[]{:S(2)}) copy-start(f32[2,20]{1,0:T(2,128)} %param.17) | copy-start | bytes 484
  142.7 0.9 copy-start.3
  145.9 118.2 %all-gather.13.cloned.1.call-start = ((), (), s32[]{:S(2)}) async-start(), calls=%async_computation.10 | async-start | bytes 2211840 | tf_op jit(solution)/shard_map/all_gather | solution.py:376
  146.0 0.9 copy-start.2
  149.2 222.4 %reduce-scatter.7.cloned.1.call-start = ((), (), s32[]{:S(2)}) async-start(), calls=%async_computation.5 | async-start | bytes 2211840 | tf_op jit(solution)/shard_map/reduce_scatter | solution.py:372
  264.0 124.9 %reduce-scatter.11.cloned.1.call-start = ((), (), s32[]{:S(2)}) async-start(), calls=%async_computation.7 | async-start | bytes 2211840 | tf_op jit(solution)/shard_map/reduce_scatter | solution.py:372
  264.1 93.3 %copy-start.6 = (f32[1,20,20,16,16]{2,4,1,3,0:T(8,128)S(1)}, f32[1,20,20,16,16]{2,4,1,3,0:T(8,128)}, u32[]{:S(2)}) copy-start(f32[1,20,20,16,16]{2,4,1,3,0:T(8,128)} %get-tuple-element.13) | copy-start | bytes 1228804
  357.1 55.0 %all-gather.11.cloned.1.call-start = ((), (), s32[]{:S(2)}) async-start(), calls=%async_computation.9 | async-start | bytes 2211840 | tf_op jit(solution)/shard_map/all_gather | solution.py:376
  371.7 0.9 copy-start.4
  374.9 91.1 %all-gather.15.cloned.1.call-start = ((), (), s32[]{:S(2)}) async-start(), calls=%async_computation.11 | async-start | bytes 2211840 | tf_op jit(solution)/shard_map/all_gather | solution.py:376
  388.9 0.9 copy-start.5
Sparse Core Ops, SparseCore 0:
  54.4 34.4 reduce-scatter.4
  92.2 33.1 reduce-scatter.8
  146.0 24.2 all-gather.8
  172.0 21.3 all-gather.12
  264.1 31.6 reduce-scatter.6
  357.2 31.6 reduce-scatter.10
  390.7 21.3 all-gather.10
  413.9 21.3 all-gather.14

commit v2 on v1

--- a/solution.py
+++ b/solution.py
@@ -12,7 +12,6 @@
 F32 = jnp.float32
 BF16 = jnp.bfloat16
 LANES = 256
-CHUNKS = 2
 PACK = 384
 
 
@@ -118,24 +117,27 @@
                 z_fwd=z_fwd, z_inv=z_inv, to_trig=sign.astype(BF16), to_modes=sign.T.astype(BF16))
 
 
-def forward_rows(v, z_fwd_ref, zs_ref, side, pair):
+def forward_rows(v, z_fwd_ref, zs_ref, ts_ref, side, pair):
     y = dot(z_fwd_ref[...], jnp.concatenate(split3(v), axis=0))
-    rows = y.shape[0] // 3
-    zs_ref[side, pair * rows:(pair + 1) * rows, :] = y[:rows] + (y[rows:2 * rows] + y[2 * rows:])
-
-
-def forward_xy(g, zs_ref, xy_ref, acc_ref):
-    plus, minus = zs_ref[0], zs_ref[1]
-    for part, v in enumerate((plus + minus, plus - minus)):
-        new = dot6(split3(v), [xy_ref[part, t, g] for t in range(3)])
-
-        @pl.when(g == 0)
-        def _():
-            acc_ref[part] = new
-
-        @pl.when(g > 0)
-        def _():
-            acc_ref[part] += new
+    size = y.shape[0] // 3
+    y = y[:size] + (y[size:2 * size] + y[2 * size:])
+    rows = slice(pair * size, (pair + 1) * size)
+    if side == 0:
+        zs_ref[rows, :] = y
+        return
+    first = zs_ref[rows, :]
+    for part, v in enumerate((first + y, first - y)):
+        for t, s in enumerate(split3(v)):
+            ts_ref[part, t, rows, :] = s
+
+
+def forward_xy(g, ts_ref, xy_ref, acc_ref):
+    @pl.when(g == 0)
+    def _():
+        acc_ref[...] = jnp.zeros_like(acc_ref)
+
+    for part in range(2):
+        acc_ref[part] += dot6([ts_ref[part, t] for t in range(3)], [xy_ref[part, t, g] for t in range(3)])
 
 
 def forward_flush(acc_ref, pq_ref, rows_ref, out_ref, width, trigs):
@@ -151,15 +153,15 @@
         out_ref[t % half, 0, (t // half) * width:(t // half + 1) * width, :] = rows_ref[:, t, :]
 
 
-def forward_kernel(width, trigs, p_ref, q_ref, z_fwd_ref, xy_ref, pq_ref, out_ref, zs_ref, acc_ref, rows_ref):
+def forward_kernel(width, trigs, p_ref, q_ref, z_fwd_ref, xy_ref, pq_ref, out_ref, zs_ref, ts_ref, acc_ref, rows_ref):
     g = pl.program_id(1)
     count = p_ref.shape[1]
     for side, ref in enumerate((p_ref, q_ref)):
         order = range(count) if side == 0 else range(count - 1, -1, -1)
         for pair in range(width // 2):
             v = jnp.concatenate([ref[0, i, 2 * pair:2 * pair + 2].reshape(-1, ref.shape[4]) for i in order], axis=1)
-            forward_rows(v, z_fwd_ref, zs_ref, side, pair)
-    forward_xy(g, zs_ref, xy_ref, acc_ref)
+            forward_rows(v, z_fwd_ref, zs_ref, ts_ref, side, pair)
+    forward_xy(g, ts_ref, xy_ref, acc_ref)
 
     @pl.when(g == pl.num_programs(1) - 1)
     def _():
@@ -181,10 +183,8 @@
             for t, s in enumerate(split3(v)):
                 gs_ref[part, t] = s
 
-    even, odd = [dot6([gs_ref[part, t] for t in range(3)], [xyt_ref[part, t, g] for t in range(3)]) for part in range(2)]
-    for side, v in enumerate((even + odd, even - odd)):
-        for t, s in enumerate(split3(v)):
-            sp_ref[side, t] = s
+    for part in range(2):
+        sp_ref[part] = dot6([gs_ref[part, t] for t in range(3)], [xyt_ref[part, t, g] for t in range(3)])
 
 
 def layer_side(side, load, mix_ref, z_inv_ref, bias_ref, sp_ref, u_ref, width, trigs, grid_z, emit):
@@ -194,7 +194,8 @@
         u_ref[:, tile * 8:(tile + 1) * 8, :] = y.reshape(width, 8, LANES)
     for pair in range(width // 2):
         rows = slice(pair * 2 * trigs, (pair + 1) * 2 * trigs)
-        y = dot(z_inv_ref[...], six_rows([sp_ref[side, t, rows, :] for t in range(3)]))
+        even, odd = sp_ref[0, rows, :], sp_ref[1, rows, :]
+        y = dot(z_inv_ref[...], six_rows(split3(even + odd if side == 0 else even - odd)))
         size = 2 * grid_z
         bias = bias_ref[pair * size:(pair + 1) * size, :]
         h = y + (u_ref[2 * pair:2 * pair + 2].reshape(size, LANES) + jnp.concatenate([bias, bias], axis=1))
@@ -202,7 +203,7 @@
 
 
 def middle_kernel(width, trigs, grid_z, p_ref, q_ref, coef_ref, mix_ref, z_inv_ref, bias_ref, z_fwd_ref, xy_ref, xyt_ref, pq_ref,
-                  v_ref, out_ref, rows_ref, gs_ref, sp_ref, u_ref, zs_ref, acc_ref):
+                  v_ref, out_ref, rows_ref, gs_ref, sp_ref, u_ref, zs_ref, ts_ref, acc_ref):
     g = pl.program_id(1)
     count = p_ref.shape[1]
     inverse_xy(g, coef_ref, pq_ref, rows_ref, gs_ref, xyt_ref, sp_ref, width, trigs)
@@ -215,10 +216,10 @@
         def emit(pair, v):
             size = 2 * grid_z
             v_ref[0, 0, side, pair * size:(pair + 1) * size, :] = v
-            forward_rows(v, z_fwd_ref, zs_ref, side, pair)
+            forward_rows(v, z_fwd_ref, zs_ref, ts_ref, side, pair)
 
         layer_side(side, load, mix_ref, z_inv_ref, bias_ref, sp_ref, u_ref, width, trigs, grid_z, emit)
-    forward_xy(g, zs_ref, xy_ref, acc_ref)
+    forward_xy(g, ts_ref, xy_ref, acc_ref)
 
     @pl.when(g == pl.num_programs(1) - 1)
     def _():
@@ -267,6 +268,22 @@
     lax.fori_loop(0, batch, one, 0)
     out = sum(dot(s, to_trig_ref[...]) for s in split3(t_ref[...].reshape(batch * rows, 2 * n))[::-1])
     out_ref[...] = out.reshape(batch, rows, PACK)
+
+
+def weights_kernel(col_devs, re_ref, im_ref, *refs):
+    outs, buf, sem = refs[:-2], refs[-2], refs[-1]
+    kz = lax.axis_index('ys') * col_devs + lax.axis_index('xs')
+    size = buf.shape[1]
+    width, _, n = outs[0].shape
+    copies = []
+    for i in range(len(outs)):
+        ref = re_ref if i % 2 == 0 else im_ref
+        copies.append(pltpu.make_async_copy(ref.at[pl.ds(i // 2 * size, size), kz], buf.at[i], sem.at[i]))
+        copies[-1].start()
+    for i, out in enumerate(outs):
+        copies[i].wait()
+        for c in range(width):
+            out[c] = buf[i, pl.ds(c, n, stride=width), 0, :].T
 
 
 def full(shape):
@@ -303,86 +320,112 @@
         eye = jnp.eye(8, dtype=F32)
         mix = [six_cols(split_xla(jnp.einsum('cd,zw->dzcw', mix_weight[l], eye, precision=lax.Precision.HIGHEST).reshape(8 * width, 8 * width))) for l in range(layers)]
         bias_rows = jnp.broadcast_to(bias[:, :, None, None], (layers, width, grid_z, 128)).reshape(layers, width * grid_z, 128)
-        kz = y_index * col_devs + x_index
-
-        def own(w):
-            w = lax.dynamic_index_in_dim(w, kz, 3, keepdims=False)
-            return jnp.transpose(w, (0, 3, 4, 1, 2)).reshape(layers, width, width, trigs * trigs)
-
-        real_w, imag_w = own(spec_real), own(spec_imag)
+        by_row = lambda w: jnp.transpose(w, (0, 1, 2, 4, 3, 5)).reshape(layers * trigs * trigs * width, modes, 1, width)
+        own = pl.pallas_call(
+            functools.partial(weights_kernel, col_devs), in_specs=[pl.BlockSpec(memory_space=pl.ANY)] * 2,
+            out_shape=[jax.ShapeDtypeStruct((width, width, trigs * trigs), F32)] * (2 * layers),
+            scratch_shapes=[pltpu.VMEM((2 * layers, trigs * trigs * width, 1, width), F32), pltpu.SemaphoreType.DMA((2 * layers,))],
+            cost_estimate=pl.CostEstimate(flops=400000000, bytes_accessed=2 ** 24, transcendentals=0),
+            compiler_params=pltpu.CompilerParams(vmem_limit_bytes=32 * 2 ** 20), name='weights')(by_row(spec_real), by_row(spec_imag))
 
         native = jnp.transpose(field, (0, 1, 4, 3, 2))
-        chunk = batch // CHUNKS
         xy_spec = full(xy.shape)
-        spectrum = jax.ShapeDtypeStruct((modes, chunk, 2 * width, PACK), F32)
-        spec_block = pl.BlockSpec((modes, 1, 2 * width, PACK), lambda b, g: (0, b, 0, 0))
-        packed = jax.ShapeDtypeStruct((chunk, groups, 2, width * grid_z, LANES), F32)
         packed_block = pl.BlockSpec((1, 1, 2, width * grid_z, LANES), lambda b, g: (b, g, 0, 0, 0))
         rows_scr = pltpu.VMEM((width, trigs, PACK), F32)
-        zs_scr = pltpu.VMEM((2, rows, LANES), F32)
+        zs_scr = pltpu.VMEM((rows, LANES), F32)
+        ts_scr = pltpu.VMEM((2, 3, rows, LANES), BF16)
         acc_scr = pltpu.VMEM((2, rows, LANES), F32)
         gs_scr = pltpu.VMEM((2, 3, rows, LANES), BF16)
-        sp_scr = pltpu.VMEM((2, 3, rows, LANES), BF16)
+        sp_scr = pltpu.VMEM((2, rows, LANES), F32)
         u_scr = pltpu.VMEM((width, grid_z, LANES), F32)
+
+        half, part = batch // 2, batch // 4
 
         def field_blocks(first):
             shape = (1, count, width, grid_z, y_loc)
             return [pl.BlockSpec(shape, lambda b, g: (first + b, g, 0, 0, 0)),
                     pl.BlockSpec(shape, lambda b, g: (first + b, 2 * groups - 1 - g, 0, 0, 0))]
 
-        def cost(us):
-            return pl.CostEstimate(flops=int(us * chunk * 4e7), bytes_accessed=chunk * 13 * 2 ** 20, transcendentals=0)
-
-        def forward(first):
-            return pl.pallas_call(
-                functools.partial(forward_kernel, width, trigs), grid=(chunk, groups),
-                in_specs=field_blocks(first) + [full(z_fwd.shape), xy_spec, full(pq.shape)],
-                out_specs=spec_block, out_shape=spectrum, scratch_shapes=[zs_scr, acc_scr, rows_scr],
-                compiler_params=params(56), cost_estimate=cost(8), name='forward')(native, native, z_fwd, xy, pq)
-
-        def middle(first, coef):
-            return pl.pallas_call(
-                functools.partial(middle_kernel, width, trigs, grid_z), grid=(chunk, groups),
-                in_specs=field_blocks(first) + [spec_block, full(mix[0].shape), full(z_inv.shape), full(bias_rows.shape[1:]), full(z_fwd.shape), xy_spec, xy_spec, full(pq.shape)],
-                out_specs=[packed_block, spec_block], out_shape=[packed, spectrum],
-                scratch_shapes=[rows_scr, gs_scr, sp_scr, u_scr, zs_scr, acc_scr],
-                compiler_params=params(60), cost_estimate=cost(22), name='middle')(
-                    native, native, coef, mix[0], z_inv, bias_rows[0], z_fwd, xy, xyt, pq)
-
-        def last(first, v, coef, out):
-            specs = [packed_block, spec_block, full(mix[1].shape), full(z_inv.shape), full(bias_rows.shape[1:]), xy_spec, full(pq.shape)]
-            args = [v, coef, mix[1], z_inv, bias_rows[1], xyt, pq]
-            kernel = functools.partial(last_kernel, width, trigs, grid_z)
-            if out is not None:
-                specs, args = [pl.BlockSpec(memory_space=pl.ANY)] + specs, [out] + args
-            body = kernel if out is None else lambda unused, *refs: kernel(*refs)
-            return pl.pallas_call(
-                body, grid=(chunk, groups), in_specs=specs,
-                out_specs=pl.BlockSpec((1, x_loc, width, grid_z, y_loc), lambda b, g: (first + b, 0, 0, 0, 0)),
+        def cost(us, n):
+            return pl.CostEstimate(flops=int(us * n * 4e7), bytes_accessed=n * 13 * 2 ** 20, transcendentals=0)
+
+        def ordered(kernel, after, specs, args, **settings):
+            extra = len(after)
+            return pl.pallas_call(lambda *refs: kernel(*refs[extra:]), in_specs=[pl.BlockSpec(memory_space=pl.ANY)] * extra + specs,
+                                  **settings)(*after, *args)
+
+        sums = jax.ShapeDtypeStruct((modes, half, 2 * width, PACK), F32)
+
+        def sums_block(at):
+            return pl.BlockSpec((modes, 1, 2 * width, PACK), lambda b, g: (0, at + b, 0, 0))
+
+        def forward(first, n, at, into, after):
+            return ordered(
+                functools.partial(forward_kernel, width, trigs), after if into is None else [into] + after,
+                field_blocks(first) + [full(z_fwd.shape), xy_spec, full(pq.shape)], [native, native, z_fwd, xy, pq],
+                grid=(n, groups), out_specs=sums_block(at), out_shape=sums, scratch_shapes=[zs_scr, ts_scr, acc_scr, rows_scr],
+                input_output_aliases={} if into is None else {0: 0},
+                compiler_params=params(56), cost_estimate=cost(8, n), name='forward')
+
+        def middle(first, n, at, coef, into, after):
+            return ordered(
+                functools.partial(middle_kernel, width, trigs, grid_z), after if into is None else [into] + after,
+                field_blocks(first) + [sums_block(at), full(mix[0].shape), full(z_inv.shape), full(bias_rows.shape[1:]), full(z_fwd.shape), xy_spec, xy_spec, full(pq.shape)],
+                [native, native, coef, mix[0], z_inv, bias_rows[0], z_fwd, xy, xyt, pq],
+                grid=(n, groups), out_specs=[packed_block, sums_block(at)],
+                out_shape=[jax.ShapeDtypeStruct((n, groups, 2, width * grid_z, LANES), F32), sums],
+                scratch_shapes=[rows_scr, gs_scr, sp_scr, u_scr, zs_scr, ts_scr, acc_scr],
+                input_output_aliases={} if into is None else {0: 1},
+                compiler_params=params(60), cost_estimate=cost(20, n), name='middle')
+
+        def last(first, n, at, v, coef, out, after):
+            first_call = out is None
+            return ordered(
+                functools.partial(last_kernel, width, trigs, grid_z), after if first_call else [out] + after,
+                [packed_block, sums_block(at), full(mix[1].shape), full(z_inv.shape), full(bias_rows.shape[1:]), xy_spec, full(pq.shape)],
+                [v, coef, mix[1], z_inv, bias_rows[1], xyt, pq],
+                grid=(n, groups), out_specs=pl.BlockSpec((1, x_loc, width, grid_z, y_loc), lambda b, g: (first + b, 0, 0, 0, 0)),
                 out_shape=jax.ShapeDtypeStruct(native.shape, F32), scratch_shapes=[rows_scr, gs_scr, sp_scr, u_scr],
-                input_output_aliases={} if out is None else {0: 0},
-                compiler_params=params(60), cost_estimate=cost(12), name='last')(*args)
-
-        mixing = pl.pallas_call(
-            functools.partial(mix_kernel, width), out_shape=jax.ShapeDtypeStruct((chunk, 2 * width, PACK), F32),
-            scratch_shapes=[pltpu.VMEM((chunk, 2 * width, 2 * trigs * trigs), F32)] * 2, cost_estimate=cost(0.3),
-            compiler_params=pltpu.CompilerParams(vmem_limit_bytes=32 * 2 ** 20), name='mixing')
+                input_output_aliases={} if first_call else {0: 0},
+                compiler_params=params(60), cost_estimate=cost(12, n), name='last')
+
+        def mixing(own_sum, layer, after):
+            n = own_sum.shape[0]
+            args = [own_sum, own[2 * layer], own[2 * layer + 1], to_modes, to_trig]
+            return ordered(
+                functools.partial(mix_kernel, width), after, [pl.BlockSpec(memory_space=pltpu.VMEM)] * len(args), args,
+                out_shape=jax.ShapeDtypeStruct((n, 2 * width, PACK), F32),
+                scratch_shapes=[pltpu.VMEM((n, 2 * width, 2 * trigs * trigs), F32)] * 2, cost_estimate=cost(0.5, n),
+                compiler_params=pltpu.CompilerParams(vmem_limit_bytes=32 * 2 ** 20), name='mixing')
 
         def gather_sum(partial):
             return lax.psum_scatter(partial, ('ys', 'xs'), scatter_dimension=0, tiled=False)
 
-        def spread(own_sum, layer):
-            mixed = mixing(own_sum, real_w[layer], imag_w[layer], to_modes, to_trig)
+        def spread(mixed):
             return lax.all_gather(mixed, ('ys', 'xs'), axis=0, tiled=False)
 
-        parts = [gather_sum(forward(i * chunk)) for i in range(CHUNKS)]
-        coefs = [spread(part, 0) for part in parts]
-        done = [middle(i * chunk, coef) for i, coef in enumerate(coefs)]
-        parts = [gather_sum(partial) for v, partial in done]
-        coefs = [spread(part, 1) for part in parts]
-        out = None
-        for i in range(CHUNKS):
-            out = last(i * chunk, done[i][0], coefs[i], out)
+        sum_a = gather_sum(forward(0, half, 0, None, []))
+        fwd_b = forward(half, part, 0, None, [])
+        mix_a = mixing(sum_a, 0, [fwd_b])
+        coef_a = spread(mix_a)
+        fwd_b = forward(half + part, part, part, fwd_b, [mix_a])
+        sum_b = gather_sum(fwd_b)
+        v_0, mid_a = middle(0, part, 0, coef_a, None, [fwd_b])
+        mix_b = mixing(sum_b, 0, [mid_a])
+        coef_b = spread(mix_b)
+        v_1, mid_a = middle(part, part, part, coef_a, mid_a, [mix_b])
+        sum_a = gather_sum(mid_a)
+        v_2, mid_b = middle(half, part, 0, coef_b, None, [mid_a])
+        mix_a = mixing(sum_a, 1, [mid_b])
+        coef_a = spread(mix_a)
+        v_3, mid_b = middle(half + part, part, part, coef_b, mid_b, [mix_a])
+        sum_b = gather_sum(mid_b)
+        out = last(0, part, 0, v_0, coef_a, None, [mid_b])
+        mix_b = mixing(sum_b, 1, [out])
+        coef_b = spread(mix_b)
+        out = last(part, part, part, v_1, coef_a, out, [mix_b])
+        out = last(half, part, 0, v_2, coef_b, out, [])
+        out = last(half + part, part, part, v_3, coef_b, out, [])
         return jnp.transpose(out, (0, 1, 4, 3, 2))
 
     field_spec = P('data', 'xs', 'ys', None, None)

time: 531 us -> 447 us (0.84)
  local copies, waits for them, and re-layouts: 85.1 us -> 26.1 us
  waiting for transfers between devices: 47.7 us -> 9.33 us
  Pallas kernels: 374 us -> 383 us
    all_gather x4, waiting for transfers between devices: 33.8 us -> 0.02 us  [spread(): return lax.all_gather(mixed, ('ys', 'xs'), axis=0, tiled=False)]
    dynamic_slice x1 -> x0, local copies, waits for them, and re-layouts: 29 us -> none  [own(): w = lax.dynamic_index_in_dim(w, kz, 3, keepdims=False)]
    slice x7 -> x1, local copies, waits for them, and re-layouts: 21.3 us -> 0.52 us  [last(): bias_rows[1]]
    squeeze x4 -> x0, local copies, waits for them, and re-layouts: 11.8 us -> none  [spread(): mixed = mixing(own_sum, real_w[layer], imag_w[layer], to_modes, to_trig)]
    pallas_call x10 -> x16, Pallas kernels: 374 us -> 383 us  [the longest x15 376 us: ordered(): pl.pallas_call(lambda *refs: kernel(*refs[extra:]), in_specs=[pl.BlockSpe...]
  transfers between devices with their start and end apart: 8 -> 8, of which waited for: 3 -> 1; matrix products, arithmetic and copies ran while one was open for 14% -> 3% of each run, Pallas kernels for 54% -> 65%
where the time goes in v2:
time: 447 us; the launch traced here: 438 us
  Pallas kernels  383 us (86%)
  local copies, waits for them, and re-layouts  26.1 us (6%)
  between operations  14.1 us (3%)
  waiting for transfers between devices  9.33 us (2%)
  other arithmetic  4.77 us (1%)
    pallas_call x15, Pallas kernels, ordered(): pl.pallas_call(lambda *refs: kernel(*refs[extra:]), in_specs=[pl.BlockSpe...  376 us
    reduce_scatter x4, waiting for transfers between devices, gather_sum(): lax.psum_scatter(partial, ('ys', 'xs'), scatter_dimension=0, tiled=False)  9.17 us
  transfers between devices with their start and end apart: 8, of which 1 were waited for; matrix products, arithmetic and copies ran while one was open for 3% of the time, Pallas kernels for 65%

profile of v2, /device:TPU:0, one launch (start us, length us, event | category | flops | bytes accessed | tf_op | source)
XLA Modules:
  0.0 438.4 jit_solution(8846431108152556430)
XLA Ops:
  9.3 1.9 copy.43
  11.9 1.9 fusion.4
  13.8 2.8 copy.44.refs_3_.refs_5_.refs_8_.refs_9_
  17.8 32.5 %forward.4 = f32[8,4,40,384]{3,2,1,0:T(8,128)} custom-call(f32[8,32,20,40,64]{4,3,2,1,0:T(8,128)} %bitcast.refs_0_.refs_1_.refs_2_.refs_3_, f32[8,32,20,40,64]{4,3,2,1,0:T(8,128)} %bitcast.refs_0_.refs_1_.refs_2_.refs_3_, bf16[96,240]{1,0:T(8,128)(2,1)} %constant.40.clone.refs_2_.refs_4_.refs_7_.refs_8_, ...), custom_call_target="tpu_custom_call" | custom-call | flops 1280000000 | bytes 54525952 | tf_op jit(solution)/shard_map/forward/pallas_call | solution.py:354
  50.3 7.4 %weights.1 = (f32[20,20,256]{2,1,0:T(8,128)S(1)}, f32[20,20,256]{2,1,0:T(8,128)S(1)}, f32[20,20,256]{2,1,0:T(8,128)S(1)}, f32[20,20,256]{2,1,0:T(8,128)S(1)}) custom-call(f32[10240,8,1,20]{3,2,1,0:T(1,128)} %bitcast.40, f32[10240,8,1,20]{3,2,1,0:T(1,128)} %bitcast.41), custom_call_target="tpu_custom_call" | custom-call | flops 400000000 | bytes 16777216 | tf_op jit(solution)/shard_map/weights/pallas_call | solution.py:324
  57.8 18.0 %forward.3.refs_0_ = f32[8,4,40,384]{3,2,1,0:T(8,128)} custom-call(f32[8,32,20,40,64]{4,3,2,1,0:T(8,128)} %bitcast.refs_0_.refs_1_.refs_2_.refs_3_, f32[8,32,20,40,64]{4,3,2,1,0:T(8,128)} %bitcast.refs_0_.refs_1_.refs_2_.refs_3_, bf16[96,240]{1,0:T(8,128)(2,1)} %constant.40.clone.refs_2_.refs_4_.refs_7_.refs_8_, ...), custom_call_target="tpu_custom_call" | custom-call | flops 640000000 | bytes 27262976 | tf_op jit(solution)/shard_map/forward/pallas_call | solution.py:354
  75.7 9.2 %reduce-scatter.5.cloned.1.call-done = f32[1,4,40,384]{3,2,1,0:T(8,128)} async-done(((f32[8,4,40,384]{3,2,1,0:T(8,128)}), f32[1,4,40,384]{3,2,1,0:T(8,128)}) %reduce-scatter.5.cloned.1.call-update) | async-done | bytes 245776 | tf_op jit(solution)/shard_map/reduce_scatter | solution.py:402
  84.9 1.5 copy-done
  87.4 2.3 mixing.4.refs_1_
  90.2 17.9 %forward.5.refs_0_ = f32[8,4,40,384]{3,2,1,0:T(8,128)} custom-call(f32[8,4,40,384]{3,2,1,0:T(8,128)} %forward.3.refs_0_, f32[4,40,384]{2,1,0:T(8,128)} %mixing.4.refs_1_, f32[8,32,20,40,64]{4,3,2,1,0:T(8,128)} %bitcast.refs_0_.refs_1_.refs_2_.refs_3_, f32[8,32,20,40,64]{4,3,2,1,0:T(8,128)} %bitcast.refs_0_.refs_1_.refs_2_.refs_3_, ...), custom_call_target="tpu_custom_call", output_to_operand_aliasing={{}: (0, {})} | custom-call | flops 640000000 | bytes 27262976 | tf_op jit(solution)/shard_map/forward/pallas_call | solution.py:354
  109.1 2.2 multiply_bitcast_fusion
  111.3 2.0 reshape.69
  115.3 45.3 %middle.4 = (f32[2,4,2,800,256]{4,3,2,1,0:T(8,128)}, f32[8,4,40,384]{3,2,1,0:T(8,128)}) custom-call(f32[8,4,40,384]{3,2,1,0:T(8,128)} %forward.5.refs_0_, f32[8,32,20,40,64]{4,3,2,1,0:T(8,128)} %bitcast.refs_0_.refs_1_.refs_2_.refs_3_, f32[8,32,20,40,64]{4,3,2,1,0:T(8,128)} %bitcast.refs_0_.refs_1_.refs_2_.refs_3_, f32[8,4,40,384]{3,2,1,0:T(8,128)} %bitcast.43, ...), custom_call_target="tpu_custom_call" | custom-call | flops 1600000000 | bytes 27262976 | tf_op jit(solution)/shard_map/middle/pallas_call | solution.py:354
  163.1 2.3 mixing.5.refs_1_
  165.6 45.4 %middle.5 = (f32[2,4,2,800,256]{4,3,2,1,0:T(8,128)}, f32[8,4,40,384]{3,2,1,0:T(8,128)}) custom-call(f32[8,4,40,384]{3,2,1,0:T(8,128)} %get-tuple-element.19.refs_0_, f32[4,40,384]{2,1,0:T(8,128)} %mixing.5.refs_1_, f32[8,32,20,40,64]{4,3,2,1,0:T(8,128)} %bitcast.refs_0_.refs_1_.refs_2_.refs_3_, ...), custom_call_target="tpu_custom_call", output_to_operand_aliasing={{1}: (0, {})} | custom-call | flops 1600000000 | bytes 27262976 | tf_op jit(solution)/shard_map/middle/pallas_call | solution.py:354
  211.1 45.3 %middle.6 = (f32[2,4,2,800,256]{4,3,2,1,0:T(8,128)}, f32[8,4,40,384]{3,2,1,0:T(8,128)}) custom-call(f32[8,4,40,384]{3,2,1,0:T(8,128)} %get-tuple-element.20.refs_0_, f32[8,32,20,40,64]{4,3,2,1,0:T(8,128)} %bitcast.refs_0_.refs_1_.refs_2_.refs_3_, f32[8,32,20,40,64]{4,3,2,1,0:T(8,128)} %bitcast.refs_0_.refs_1_.refs_2_.refs_3_, f32[8,4,40,384]{3,2,1,0:T(8,128)} %bitcast.45, ...), custom_call_target="tpu_custom_call" | custom-call | flops 1600000000 | bytes 27262976 | tf_op jit(solution)/shard_map/middle/pallas_call | solution.py:354
  258.9 2.3 mixing.6.refs_1_
  261.3 45.3 %middle.7 = (f32[2,4,2,800,256]{4,3,2,1,0:T(8,128)}, f32[8,4,40,384]{3,2,1,0:T(8,128)}) custom-call(f32[8,4,40,384]{3,2,1,0:T(8,128)} %get-tuple-element.21.refs_0_, f32[4,40,384]{2,1,0:T(8,128)} %mixing.6.refs_1_, f32[8,32,20,40,64]{4,3,2,1,0:T(8,128)} %bitcast.refs_0_.refs_1_.refs_2_.refs_3_, ...), custom_call_target="tpu_custom_call", output_to_operand_aliasing={{1}: (0, {})} | custom-call | flops 1600000000 | bytes 27262976 | tf_op jit(solution)/shard_map/middle/pallas_call | solution.py:354
  307.0 2.0 reshape.70
  311.0 29.2 %last.4.refs_0_ = f32[8,32,20,40,64]{4,3,2,1,0:T(8,128)} custom-call(f32[8,4,40,384]{3,2,1,0:T(8,128)} %get-tuple-element.24.refs_0_, f32[2,4,2,800,256]{4,3,2,1,0:T(8,128)} %get-tuple-element.25.refs_1_, f32[8,4,40,384]{3,2,1,0:T(8,128)} %bitcast.49, bf16[160,960]{1,0:T(8,128)(2,1)} %concatenate.7.refs_3_.refs_4_, ...), custom_call_target="tpu_custom_call" | custom-call | flops 960000000 | bytes 27262976 | tf_op jit(solution)/shard_map/last/pallas_call | solution.py:354
  341.2 2.3 mixing.7.refs_1_
  343.5 29.2 %last.5.refs_0_ = f32[8,32,20,40,64]{4,3,2,1,0:T(8,128)} custom-call(f32[8,32,20,40,64]{4,3,2,1,0:T(8,128)} %last.4.refs_0_, f32[4,40,384]{2,1,0:T(8,128)} %mixing.7.refs_1_, f32[2,4,2,800,256]{4,3,2,1,0:T(8,128)} %get-tuple-element.26.refs_2_, f32[8,4,40,384]{3,2,1,0:T(8,128)} %bitcast.50, ...), custom_call_target="tpu_custom_call", output_to_operand_aliasing={{}: (0, {})} | custom-call | flops 960000000 | bytes 27262976 | tf_op jit(solution)/shard_map/last/pallas_call | solution.py:354
  372.7 29.2 %last.6.refs_0_ = f32[8,32,20,40,64]{4,3,2,1,0:T(8,128)} custom-call(f32[8,32,20,40,64]{4,3,2,1,0:T(8,128)} %last.5.refs_0_, f32[2,4,2,800,256]{4,3,2,1,0:T(8,128)} %get-tuple-element.27.refs_1_, f32[8,4,40,384]{3,2,1,0:T(8,128)} %bitcast.47, bf16[160,960]{1,0:T(8,128)(2,1)} %concatenate.7.refs_3_.refs_4_, ...), custom_call_target="tpu_custom_call", output_to_operand_aliasing={{}: (0, {})} | custom-call | flops 960000000 | bytes 27262976 | tf_op jit(solution)/shard_map/last/pallas_call | solution.py:354
  402.0 29.3 %last.7 = f32[8,32,20,40,64]{4,3,2,1,0:T(8,128)} custom-call(f32[8,32,20,40,64]{4,3,2,1,0:T(8,128)} %last.6.refs_0_, f32[2,4,2,800,256]{4,3,2,1,0:T(8,128)} %get-tuple-element.28.refs_1_, f32[8,4,40,384]{3,2,1,0:T(8,128)} %bitcast.48, bf16[160,960]{1,0:T(8,128)(2,1)} %concatenate.7.refs_3_.refs_4_, ...), custom_call_target="tpu_custom_call", output_to_operand_aliasing={{}: (0, {})} | custom-call | flops 960000000 | bytes 27262976 | tf_op jit(solution)/shard_map/last/pallas_call | solution.py:354
  (69 shorter events, 17.8 us)
Async XLA Ops:
  6.5 1.3 copy-start.9
  6.5 78.4 %reduce-scatter.5.cloned.1.call-start = ((), (), s32[]{:S(2)}) async-start(), calls=%async_computation.4 | async-start | bytes 2211840 | tf_op jit(solution)/shard_map/reduce_scatter | solution.py:402
  50.3 64.1 %all-gather.9.cloned.1.call-start = ((), (), s32[]{:S(2)}) async-start(), calls=%async_computation.8 | async-start | bytes 2211840 | tf_op jit(solution)/shard_map/all_gather | solution.py:405
  57.8 27.1 %copy-start.3 = (bf16[512,384]{1,0:T(8,128)(2,1)S(1)}, bf16[512,384]{1,0:T(8,128)(2,1)}, u32[]{:S(2)}) copy-start(bf16[512,384]{1,0:T(8,128)(2,1)} %constant.43.clone.refs_5_) | copy-start | bytes 1179652
  57.8 27.1 %copy-start.4 = (bf16[384,512]{1,0:T(8,128)(2,1)S(1)}, bf16[384,512]{1,0:T(8,128)(2,1)}, u32[]{:S(2)}) copy-start(bf16[384,512]{1,0:T(8,128)(2,1)} %constant.42.clone.refs_4_) | copy-start | bytes 1179652
  84.9 1.5 copy-start
  86.5 0.9 copy-start.8
  89.7 18.5 %copy-start.12 = (f32[2,20]{1,0:T(2,128)S(1)}, f32[2,20]{1,0:T(2,128)}, u32[]{:S(2)}) copy-start(f32[2,20]{1,0:T(2,128)} %param.17) | copy-start | bytes 484
  89.7 19.2 %copy-start.10 = (f32[2,20,20]{2,0,1:T(2,128)S(1)}, f32[2,20,20]{2,0,1:T(2,128)}, u32[]{:S(2)}) copy-start(f32[2,20,20]{2,0,1:T(2,128)} %param.16) | copy-start | bytes 9604
  89.7 70.9 %reduce-scatter.7.cloned.1.call-start = ((), (), s32[]{:S(2)}) async-start(), calls=%async_computation.5 | async-start | bytes 2211840 | tf_op jit(solution)/shard_map/reduce_scatter | solution.py:402
  108.1 103.0 %all-gather.11.cloned.1.call-start = ((), (), s32[]{:S(2)}) async-start(), calls=%async_computation.9 | async-start | bytes 2211840 | tf_op jit(solution)/shard_map/all_gather | solution.py:405
  160.6 1.5 copy-start.1
  162.1 0.9 copy-start.6
  165.4 91.0 %reduce-scatter.9.cloned.1.call-start = ((), (), s32[]{:S(2)}) async-start(), calls=%async_computation.6 | async-start | bytes 2211840 | tf_op jit(solution)/shard_map/reduce_scatter | solution.py:402
  211.0 99.0 %all-gather.13.cloned.1.call-start = ((), (), s32[]{:S(2)}) async-start(), calls=%async_computation.10 | async-start | bytes 2211840 | tf_op jit(solution)/shard_map/all_gather | solution.py:405
  256.4 1.5 copy-start.2
  258.0 0.9 copy-start.7
  261.2 45.7 %copy-start.11 = (f32[20]{0:T(128)S(1)}, f32[20]{0:T(128)}, u32[]{:S(2)}) copy-start(f32[20]{0:T(128)} %get-tuple-element.44) | copy-start | bytes 244
  261.2 79.0 %reduce-scatter.11.cloned.1.call-start = ((), (), s32[]{:S(2)}) async-start(), calls=%async_computation.7 | async-start | bytes 2211840 | tf_op jit(solution)/shard_map/reduce_scatter | solution.py:402
  306.6 66.1 %all-gather.15.cloned.1.call-start = ((), (), s32[]{:S(2)}) async-start(), calls=%async_computation.11 | async-start | bytes 2211840 | tf_op jit(solution)/shard_map/all_gather | solution.py:405
  340.2 0.9 copy-start.5
Sparse Core Ops, SparseCore 0:
  50.4 34.4 reduce-scatter.4
  89.8 21.4 all-gather.8
  114.6 31.6 reduce-scatter.6
  165.5 21.4 all-gather.10
  211.2 31.6 reduce-scatter.8
  261.3 21.4 all-gather.12
  306.7 31.6 reduce-scatter.10
  343.6 21.3 all-gather.14

commit v3 on v2

--- a/solution.py
+++ b/solution.py
@@ -51,6 +51,11 @@
 
 def six_cols(s, xp=jnp):
     return xp.concatenate([s[0], s[1], s[2], s[0], s[1], s[0]], axis=1)
+
+
+def gelu(h):
+    c = math.sqrt(2.0 / math.pi)
+    return (0.5 * h) * (1.0 + jnp.tanh(h * (c + (c * 0.044715) * (h * h))))
 
 
 def lane_map(modes):
@@ -180,45 +185,56 @@
         a = jnp.concatenate([packed[:, :128], tail], axis=1)
         b = jnp.concatenate([packed[:, 128:256], pltpu.roll(tail, 64, 1)], axis=1)
         for part, v in enumerate((p * a + q * b, p * b - q * a)):
-            for t, s in enumerate(split3(v)):
-                gs_ref[part, t] = s
+            hi, mid, lo = split3(v)
+            for i, s in enumerate((hi, hi, hi, mid, mid, lo)):
+                gs_ref[part, :, i * 128:(i + 1) * 128] = s[:, :128]
+            hi, mid, lo = [s[:, 128:].astype(F32) for s in (hi, mid, lo)]
+            tail = (hi + pltpu.roll(hi, 32, 1)) + (pltpu.roll(hi, 64, 1) + pltpu.roll(mid, 96, 1))
+            gs_ref[part, :, 768:896] = tail.astype(BF16)
+            gs_ref[part, :, 896:1024] = (mid + pltpu.roll(lo, 32, 1)).astype(BF16)
 
     for part in range(2):
-        sp_ref[part] = dot6([gs_ref[part, t] for t in range(3)], [xyt_ref[part, t, g] for t in range(3)])
-
-
-def layer_side(side, load, mix_ref, z_inv_ref, bias_ref, sp_ref, u_ref, width, trigs, grid_z, emit):
-    for tile in range(grid_z // 8):
-        v = load(tile)
-        y = dot(mix_ref[...], six_rows(split3(v)))
-        u_ref[:, tile * 8:(tile + 1) * 8, :] = y.reshape(width, 8, LANES)
-    for pair in range(width // 2):
-        rows = slice(pair * 2 * trigs, (pair + 1) * 2 * trigs)
-        even, odd = sp_ref[0, rows, :], sp_ref[1, rows, :]
-        y = dot(z_inv_ref[...], six_rows(split3(even + odd if side == 0 else even - odd)))
-        size = 2 * grid_z
-        bias = bias_ref[pair * size:(pair + 1) * size, :]
-        h = y + (u_ref[2 * pair:2 * pair + 2].reshape(size, LANES) + jnp.concatenate([bias, bias], axis=1))
-        emit(pair, jax.nn.gelu(h, approximate=True))
-
-
-def middle_kernel(width, trigs, grid_z, p_ref, q_ref, coef_ref, mix_ref, z_inv_ref, bias_ref, z_fwd_ref, xy_ref, xyt_ref, pq_ref,
+        sp_ref[part] = dot(gs_ref[part], xyt_ref[part, g])
+
+
+def layer_sides(loads, mix_ref, z_inv_ref, sp_ref, u_ref, width, trigs, grid_z, emit, mingle):
+    ones = jnp.ones((16, LANES), BF16)
+    tiles = grid_z // 8
+
+    def pointwise(side, tile):
+        y = dot(mix_ref[...], jnp.concatenate([six_rows(split3(loads[side](tile))), ones], axis=0))
+        u_ref[side, :, tile * 8:(tile + 1) * 8, :] = y.reshape(width, 8, LANES)
+
+    for tile in range(tiles):
+        pointwise(0, tile)
+    for side in range(2):
+        first = 0 if not mingle else min(tiles, (width // 2 + 1) // 2)
+        for tile in range(first, tiles if side == 1 else first):
+            pointwise(1, tile)
+        for pair in range(width // 2):
+            rows = slice(pair * 2 * trigs, (pair + 1) * 2 * trigs)
+            even, odd = sp_ref[0, rows, :], sp_ref[1, rows, :]
+            y = dot(z_inv_ref[...], six_rows(split3(even + odd if side == 0 else even - odd)))
+            if mingle and side == 0 and pair % 2 == 0 and pair // 2 < tiles:
+                pointwise(1, pair // 2)
+            emit(side, pair, gelu(y + u_ref[side, 2 * pair:2 * pair + 2].reshape(2 * grid_z, LANES)))
+
+
+def middle_kernel(width, trigs, grid_z, p_ref, q_ref, coef_ref, mix_ref, z_inv_ref, z_fwd_ref, xy_ref, xyt_ref, pq_ref,
                   v_ref, out_ref, rows_ref, gs_ref, sp_ref, u_ref, zs_ref, ts_ref, acc_ref):
     g = pl.program_id(1)
     count = p_ref.shape[1]
     inverse_xy(g, coef_ref, pq_ref, rows_ref, gs_ref, xyt_ref, sp_ref, width, trigs)
-    for side, ref in enumerate((p_ref, q_ref)):
-        order = range(count) if side == 0 else range(count - 1, -1, -1)
-
-        def load(tile):
-            return jnp.concatenate([ref[0, i, :, tile * 8:(tile + 1) * 8, :].reshape(8 * width, -1) for i in order], axis=1)
-
-        def emit(pair, v):
-            size = 2 * grid_z
-            v_ref[0, 0, side, pair * size:(pair + 1) * size, :] = v
-            forward_rows(v, z_fwd_ref, zs_ref, ts_ref, side, pair)
-
-        layer_side(side, load, mix_ref, z_inv_ref, bias_ref, sp_ref, u_ref, width, trigs, grid_z, emit)
+    def load(ref, order, tile):
+        return jnp.concatenate([ref[0, i, :, tile * 8:(tile + 1) * 8, :].reshape(8 * width, -1) for i in order], axis=1)
+
+    def emit(side, pair, v):
+        size = 2 * grid_z
+        v_ref[0, 0, side, pair * size:(pair + 1) * size, :] = v
+        forward_rows(v, z_fwd_ref, zs_ref, ts_ref, side, pair)
+
+    loads = [functools.partial(load, p_ref, range(count)), functools.partial(load, q_ref, range(count - 1, -1, -1))]
+    layer_sides(loads, mix_ref, z_inv_ref, sp_ref, u_ref, width, trigs, grid_z, emit, True)
     forward_xy(g, ts_ref, xy_ref, acc_ref)
 
     @pl.when(g == pl.num_programs(1) - 1)
@@ -226,23 +242,23 @@
         forward_flush(acc_ref, pq_ref, rows_ref, out_ref, width, trigs)
 
 
-def last_kernel(width, trigs, grid_z, v_ref, coef_ref, mix_ref, z_inv_ref, bias_ref, xyt_ref, pq_ref,
+def last_kernel(width, trigs, grid_z, v_ref, coef_ref, mix_ref, z_inv_ref, xyt_ref, pq_ref,
                 out_ref, rows_ref, gs_ref, sp_ref, u_ref):
     g = pl.program_id(1)
     y_loc = out_ref.shape[4]
     count = LANES // y_loc
     inverse_xy(g, coef_ref, pq_ref, rows_ref, gs_ref, xyt_ref, sp_ref, width, trigs)
-    for side in range(2):
-        def load(tile):
-            v = v_ref[0, 0, side].reshape(width, grid_z, LANES)[:, tile * 8:(tile + 1) * 8, :]
-            return v.reshape(width * 8, LANES)
-
-        def emit(pair, v):
-            for i in range(count):
-                x = count * g + i if side == 0 else out_ref.shape[1] - 1 - count * g - i
-                out_ref[0, x, 2 * pair:2 * pair + 2] = v[:, i * y_loc:(i + 1) * y_loc].reshape(2, grid_z, y_loc)
-
-        layer_side(side, load, mix_ref, z_inv_ref, bias_ref, sp_ref, u_ref, width, trigs, grid_z, emit)
+    def load(side, tile):
+        v = v_ref[0, 0, side].reshape(width, grid_z, LANES)[:, tile * 8:(tile + 1) * 8, :]
+        return v.reshape(width * 8, LANES)
+
+    def emit(side, pair, v):
+        for i in range(count):
+            x = count * g + i if side == 0 else out_ref.shape[1] - 1 - count * g - i
+            out_ref[0, x, 2 * pair:2 * pair + 2] = v[:, i * y_loc:(i + 1) * y_loc].reshape(2, grid_z, y_loc)
+
+    loads = [functools.partial(load, side) for side in range(2)]
+    layer_sides(loads, mix_ref, z_inv_ref, sp_ref, u_ref, width, trigs, grid_z, emit, False)
 
 
 def mix_kernel(width, in_ref, re_ref, im_ref, to_modes_ref, to_trig_ref, out_ref, f_ref, t_ref):
@@ -284,6 +300,32 @@
         copies[i].wait()
         for c in range(width):
             out[c] = buf[i, pl.ds(c, n, stride=width), 0, :].T
+
+
+def tables_kernel(x_ref, y_ref, w_ref, bias_ref, spread_ref, pick_ref, xyt_ref, *mix_refs):
+    groups = xyt_ref.shape[1]
+    y_loc = y_ref.shape[1]
+    count = LANES // y_loc
+    for part in range(2):
+        for g in range(groups):
+            v = jnp.concatenate([x_ref[part, :, g * count + i:g * count + i + 1] * y_ref[...] for i in range(count)], axis=1)
+            terms = split3(v)
+            for i, t in enumerate((0, 1, 2, 0, 1, 0)):
+                xyt_ref[part, g, i * 128:(i + 1) * 128, :] = terms[t][:128]
+                xyt_ref[part, g, 768 + i * 32:768 + (i + 1) * 32, :] = terms[t][128:160]
+            xyt_ref[part, g, 960:, :] = jnp.zeros((64, LANES), BF16)
+    spread = spread_ref[...]
+    for layer, mix_ref in enumerate(mix_refs):
+        rows, columns = mix_ref.shape
+        six = jnp.zeros((rows, columns), F32)
+        for t, s in enumerate(split3(w_ref[layer])):
+            by_row = lax.dot_general(spread, s, (((1,), (1,)), ((), ())), preferred_element_type=F32).astype(BF16)
+            six += dot(by_row, pick_ref[t])
+        row, column = [lax.broadcasted_iota(jnp.int32, (rows, columns), d) for d in range(2)]
+        six = jnp.where((row - column) % 8 == 0, six, 0.0)
+        for t, s in enumerate(split3(bias_ref[layer])):
+            six = jnp.where(column == 6 * rows + t, dot(spread, jnp.broadcast_to(s, (s.shape[0], 128)))[:, :1], six)
+        mix_ref[...] = six.astype(BF16)
 
 
 def full(shape):
@@ -314,12 +356,16 @@
         trig_x = jnp.stack([jnp.asarray(t['cos_u']), jnp.asarray(t['sin_u'])])
         xy = (trig_x[:, :, None, :] * trig_y[None, None]).reshape(2, groups, LANES, LANES)
         xy = jnp.stack(split_xla(xy), axis=1)
-        xyt = jnp.swapaxes(xy, 3, 4)
         z_fwd, z_inv = jnp.asarray(t['z_fwd']), jnp.asarray(t['z_inv'])
         to_modes, to_trig = jnp.asarray(t['to_modes']), jnp.asarray(t['to_trig'])
-        eye = jnp.eye(8, dtype=F32)
-        mix = [six_cols(split_xla(jnp.einsum('cd,zw->dzcw', mix_weight[l], eye, precision=lax.Precision.HIGHEST).reshape(8 * width, 8 * width))) for l in range(layers)]
-        bias_rows = jnp.broadcast_to(bias[:, :, None, None], (layers, width, grid_z, 128)).reshape(layers, width * grid_z, 128)
+        trig_yt = lax.dynamic_index_in_dim(jnp.asarray(np.swapaxes(t['trig_y'], 1, 2)), y_index, 0, keepdims=False)
+        trig_xt = jnp.asarray(np.swapaxes(np.stack([t['cos_u'], t['sin_u']]), 1, 2))
+        spread_rows = np.kron(np.eye(width), np.ones((8, 1)))
+        pick = np.zeros((3, width, 48 * width + 16))
+        for i, term in enumerate((0, 1, 2, 0, 1, 0)):
+            pick[term, :, i * 8 * width:(i + 1) * 8 * width] = spread_rows.T
+        spread_rows, pick = jnp.asarray(spread_rows, BF16), jnp.asarray(pick, BF16)
+
         by_row = lambda w: jnp.transpose(w, (0, 1, 2, 4, 3, 5)).reshape(layers * trigs * trigs * width, modes, 1, width)
         own = pl.pallas_call(
             functools.partial(weights_kernel, col_devs), in_specs=[pl.BlockSpec(memory_space=pl.ANY)] * 2,
@@ -335,9 +381,9 @@
         zs_scr = pltpu.VMEM((rows, LANES), F32)
         ts_scr = pltpu.VMEM((2, 3, rows, LANES), BF16)
         acc_scr = pltpu.VMEM((2, rows, LANES), F32)
-        gs_scr = pltpu.VMEM((2, 3, rows, LANES), BF16)
+        gs_scr = pltpu.VMEM((2, rows, 4 * LANES), BF16)
         sp_scr = pltpu.VMEM((2, rows, LANES), F32)
-        u_scr = pltpu.VMEM((width, grid_z, LANES), F32)
+        u_scr = pltpu.VMEM((2, width, grid_z, LANES), F32)
 
         half, part = batch // 2, batch // 4
 
@@ -370,8 +416,8 @@
         def middle(first, n, at, coef, into, after):
             return ordered(
                 functools.partial(middle_kernel, width, trigs, grid_z), after if into is None else [into] + after,
-                field_blocks(first) + [sums_block(at), full(mix[0].shape), full(z_inv.shape), full(bias_rows.shape[1:]), full(z_fwd.shape), xy_spec, xy_spec, full(pq.shape)],
-                [native, native, coef, mix[0], z_inv, bias_rows[0], z_fwd, xy, xyt, pq],
+                field_blocks(first) + [sums_block(at), full(mix[0].shape), full(z_inv.shape), full(z_fwd.shape), xy_spec, full(xyt.shape), full(pq.shape)],
+                [native, native, coef, mix[0], z_inv, z_fwd, xy, xyt, pq],
                 grid=(n, groups), out_specs=[packed_block, sums_block(at)],
                 out_shape=[jax.ShapeDtypeStruct((n, groups, 2, width * grid_z, LANES), F32), sums],
                 scratch_shapes=[rows_scr, gs_scr, sp_scr, u_scr, zs_scr, ts_scr, acc_scr],
@@ -382,12 +428,20 @@
             first_call = out is None
             return ordered(
                 functools.partial(last_kernel, width, trigs, grid_z), after if first_call else [out] + after,
-                [packed_block, sums_block(at), full(mix[1].shape), full(z_inv.shape), full(bias_rows.shape[1:]), xy_spec, full(pq.shape)],
-                [v, coef, mix[1], z_inv, bias_rows[1], xyt, pq],
+                [packed_block, sums_block(at), full(mix[1].shape), full(z_inv.shape), full(xyt.shape), full(pq.shape)],
+                [v, coef, mix[1], z_inv, xyt, pq],
                 grid=(n, groups), out_specs=pl.BlockSpec((1, x_loc, width, grid_z, y_loc), lambda b, g: (first + b, 0, 0, 0, 0)),
                 out_shape=jax.ShapeDtypeStruct(native.shape, F32), scratch_shapes=[rows_scr, gs_scr, sp_scr, u_scr],
                 input_output_aliases={} if first_call else {0: 0},
                 compiler_params=params(60), cost_estimate=cost(12, n), name='last')
+
+        def make_tables(after):
+            args = [trig_xt, trig_yt, mix_weight, bias[:, :, None], spread_rows, pick]
+            shapes = [(2, groups, 4 * LANES, LANES)] + [(8 * width, 48 * width + 16)] * layers
+            return ordered(
+                tables_kernel, after, [pl.BlockSpec(memory_space=pltpu.VMEM)] * len(args), args,
+                out_shape=[jax.ShapeDtypeStruct(shape, BF16) for shape in shapes], cost_estimate=cost(1, 4),
+                compiler_params=pltpu.CompilerParams(vmem_limit_bytes=32 * 2 ** 20), name='tables')
 
         def mixing(own_sum, layer, after):
             n = own_sum.shape[0]
@@ -406,7 +460,8 @@
 
         sum_a = gather_sum(forward(0, half, 0, None, []))
         fwd_b = forward(half, part, 0, None, [])
-        mix_a = mixing(sum_a, 0, [fwd_b])
+        xyt, *mix = make_tables([fwd_b])
+        mix_a = mixing(sum_a, 0, [mix[0]])
         coef_a = spread(mix_a)
         fwd_b = forward(half + part, part, part, fwd_b, [mix_a])
         sum_b = gather_sum(fwd_b)

time: 447 us -> 412 us (0.922); the launches traced: 438 us -> 409 us
  Pallas kernels: 383 us -> 366 us
  local copies, waits for them, and re-layouts: 26.1 us -> 14.3 us
    pallas_call x15 -> x16, Pallas kernels: 376 us -> 359 us  [ordered(): pl.pallas_call(lambda *refs: kernel(*refs[extra:]), in_specs=[pl.BlockSpe...]
    unnamed x26 -> x37, local copies, waits for them, and re-layouts: 8.44 us -> 11.1 us
  transfers between devices with their start and end apart: 8 -> 8, of which waited for: 1 -> 3; matrix products, arithmetic and copies ran while one was open for 3% -> 0% of each run, Pallas kernels for 65% -> 66%
where the time goes in v3:
time: 412 us; the launch traced here: 409 us
  Pallas kernels  366 us (89%)
  local copies, waits for them, and re-layouts  14.3 us (3%)
  between operations  13.9 us (3%)
  waiting for transfers between devices  10.2 us (2%)
    pallas_call x16, Pallas kernels, ordered(): pl.pallas_call(lambda *refs: kernel(*refs[extra:]), in_specs=[pl.BlockSpe...  359 us
    unnamed x37, local copies, waits for them, and re-layouts  11.1 us
  transfers between devices with their start and end apart: 8, of which 3 were waited for; matrix products, arithmetic and copies ran while one was open for 0% of the time, Pallas kernels for 66%

profile of v3, /device:TPU:0, one launch (start us, length us, event | category | flops | bytes accessed | tf_op | source)
XLA Modules:
  0.0 409.1 jit_solution(5382529868918211345)
XLA Ops:
  10.3 2.0 pad_maximum_fusion.refs_3_.refs_5_.refs_7_.refs_8_
  12.3 32.5 %forward.4 = f32[8,4,40,384]{3,2,1,0:T(8,128)} custom-call(f32[8,32,20,40,64]{4,3,2,1,0:T(8,128)} %bitcast.refs_0_.refs_1_.refs_2_.refs_3_, f32[8,32,20,40,64]{4,3,2,1,0:T(8,128)} %bitcast.refs_0_.refs_1_.refs_2_.refs_3_, bf16[96,240]{1,0:T(8,128)(2,1)} %constant.52.clone.refs_2_.refs_4_.refs_6_.refs_7_, ...), custom_call_target="tpu_custom_call" | custom-call | flops 1280000000 | bytes 54525952 | tf_op jit(solution)/shard_map/forward/pallas_call | solution.py:400
  45.6 17.9 %forward.3.refs_0_ = f32[8,4,40,384]{3,2,1,0:T(8,128)} custom-call(f32[8,32,20,40,64]{4,3,2,1,0:T(8,128)} %bitcast.refs_0_.refs_1_.refs_2_.refs_3_, f32[8,32,20,40,64]{4,3,2,1,0:T(8,128)} %bitcast.refs_0_.refs_1_.refs_2_.refs_3_, bf16[96,240]{1,0:T(8,128)(2,1)} %constant.52.clone.refs_2_.refs_4_.refs_6_.refs_7_, ...), custom_call_target="tpu_custom_call" | custom-call | flops 640000000 | bytes 27262976 | tf_op jit(solution)/shard_map/forward/pallas_call | solution.py:400
  65.1 1.9 tables.1
  67.1 2.0 copy-done
  69.8 7.6 %weights.1 = (f32[20,20,256]{2,1,0:T(8,128)S(1)}, f32[20,20,256]{2,1,0:T(8,128)S(1)}, f32[20,20,256]{2,1,0:T(8,128)S(1)}, f32[20,20,256]{2,1,0:T(8,128)S(1)}) custom-call(f32[10240,8,1,20]{3,2,1,0:T(1,128)} %bitcast.29, f32[10240,8,1,20]{3,2,1,0:T(1,128)} %bitcast.30), custom_call_target="tpu_custom_call" | custom-call | flops 400000000 | bytes 16777216 | tf_op jit(solution)/shard_map/weights/pallas_call | solution.py:370
  77.3 2.1 reduce-scatter.5.cloned.1.call-done
  80.4 2.3 mixing.4.refs_1_
  82.8 17.9 %forward.5.refs_0_ = f32[8,4,40,384]{3,2,1,0:T(8,128)} custom-call(f32[8,4,40,384]{3,2,1,0:T(8,128)} %forward.3.refs_0_, f32[4,40,384]{2,1,0:T(8,128)} %mixing.4.refs_1_, f32[8,32,20,40,64]{4,3,2,1,0:T(8,128)} %bitcast.refs_0_.refs_1_.refs_2_.refs_3_, f32[8,32,20,40,64]{4,3,2,1,0:T(8,128)} %bitcast.refs_0_.refs_1_.refs_2_.refs_3_, ...), custom_call_target="tpu_custom_call", output_to_operand_aliasing={{}: (0, {})} | custom-call | flops 640000000 | bytes 27262976 | tf_op jit(solution)/shard_map/forward/pallas_call | solution.py:400
  100.9 4.2 %all-gather.9.cloned.1.call-done = f32[32,40,384]{2,1,0:T(8,128)} async-done(((f32[4,40,384]{2,1,0:T(8,128)}), f32[32,40,384]{2,1,0:T(8,128)}) %all-gather.9.cloned.1.call-update) | async-done | bytes 1966096 | tf_op jit(solution)/shard_map/all_gather | solution.py:459
  105.0 42.1 %middle.4 = (f32[2,4,2,800,256]{4,3,2,1,0:T(8,128)}, f32[8,4,40,384]{3,2,1,0:T(8,128)}) custom-call(f32[8,4,40,384]{3,2,1,0:T(8,128)} %forward.5.refs_0_, f32[8,32,20,40,64]{4,3,2,1,0:T(8,128)} %bitcast.refs_0_.refs_1_.refs_2_.refs_3_, f32[8,32,20,40,64]{4,3,2,1,0:T(8,128)} %bitcast.refs_0_.refs_1_.refs_2_.refs_3_, f32[8,4,40,384]{3,2,1,0:T(8,128)} %bitcast.38, ...), custom_call_target="tpu_custom_call" | custom-call | flops 1600000000 | bytes 27262976 | tf_op jit(solution)/shard_map/middle/pallas_call | solution.py:400
  147.1 1.5 copy-done.3
  149.6 2.3 mixing.5.refs_1_
  151.9 42.3 %middle.5 = (f32[2,4,2,800,256]{4,3,2,1,0:T(8,128)}, f32[8,4,40,384]{3,2,1,0:T(8,128)}) custom-call(f32[8,4,40,384]{3,2,1,0:T(8,128)} %get-tuple-element.24.refs_0_, f32[4,40,384]{2,1,0:T(8,128)} %mixing.5.refs_1_, f32[8,32,20,40,64]{4,3,2,1,0:T(8,128)} %bitcast.refs_0_.refs_1_.refs_2_.refs_3_, ...), custom_call_target="tpu_custom_call", output_to_operand_aliasing={{1}: (0, {})} | custom-call | flops 1600000000 | bytes 27262976 | tf_op jit(solution)/shard_map/middle/pallas_call | solution.py:400
  194.5 42.1 %middle.6 = (f32[2,4,2,800,256]{4,3,2,1,0:T(8,128)}, f32[8,4,40,384]{3,2,1,0:T(8,128)}) custom-call(f32[8,4,40,384]{3,2,1,0:T(8,128)} %get-tuple-element.25.refs_0_, f32[8,32,20,40,64]{4,3,2,1,0:T(8,128)} %bitcast.refs_0_.refs_1_.refs_2_.refs_3_, f32[8,32,20,40,64]{4,3,2,1,0:T(8,128)} %bitcast.refs_0_.refs_1_.refs_2_.refs_3_, f32[8,4,40,384]{3,2,1,0:T(8,128)} %bitcast.36, ...), custom_call_target="tpu_custom_call" | custom-call | flops 1600000000 | bytes 27262976 | tf_op jit(solution)/shard_map/middle/pallas_call | solution.py:400
  236.7 1.5 copy-done.2
  239.2 2.3 mixing.6.refs_1_
  241.5 42.2 %middle.7 = (f32[2,4,2,800,256]{4,3,2,1,0:T(8,128)}, f32[8,4,40,384]{3,2,1,0:T(8,128)}) custom-call(f32[8,4,40,384]{3,2,1,0:T(8,128)} %get-tuple-element.26.refs_0_, f32[4,40,384]{2,1,0:T(8,128)} %mixing.6.refs_1_, f32[8,32,20,40,64]{4,3,2,1,0:T(8,128)} %bitcast.refs_0_.refs_1_.refs_2_.refs_3_, ...), custom_call_target="tpu_custom_call", output_to_operand_aliasing={{1}: (0, {})} | custom-call | flops 1600000000 | bytes 27262976 | tf_op jit(solution)/shard_map/middle/pallas_call | solution.py:400
  284.1 27.7 %last.4.refs_0_ = f32[8,32,20,40,64]{4,3,2,1,0:T(8,128)} custom-call(f32[8,4,40,384]{3,2,1,0:T(8,128)} %get-tuple-element.29.refs_0_, f32[2,4,2,800,256]{4,3,2,1,0:T(8,128)} %get-tuple-element.30.refs_1_, f32[8,4,40,384]{3,2,1,0:T(8,128)} %bitcast.32, bf16[160,976]{1,0:T(8,128)(2,1)} %copy-done.7, bf16[80,192]{1,0:T(8,128)(2,1)} %constant.53.clone.refs_5_.refs_6_.refs_4_, ...), custom_call_target="tpu_custom_call" | custom-call | flops 960000000 | bytes 27262976 | tf_op jit(solution)/shard_map/last/pallas_call | solution.py:400
  311.8 3.8 reduce-scatter.11.cloned.1.call-done
  316.5 2.3 mixing.7.refs_1_
  318.8 27.7 %last.5.refs_0_ = f32[8,32,20,40,64]{4,3,2,1,0:T(8,128)} custom-call(f32[8,32,20,40,64]{4,3,2,1,0:T(8,128)} %last.4.refs_0_, f32[4,40,384]{2,1,0:T(8,128)} %mixing.7.refs_1_, f32[2,4,2,800,256]{4,3,2,1,0:T(8,128)} %get-tuple-element.32.refs_2_, f32[8,4,40,384]{3,2,1,0:T(8,128)} %bitcast.33, ...), custom_call_target="tpu_custom_call", output_to_operand_aliasing={{}: (0, {})} | custom-call | flops 960000000 | bytes 27262976 | tf_op jit(solution)/shard_map/last/pallas_call | solution.py:400
  346.5 27.7 %last.6.refs_0_ = f32[8,32,20,40,64]{4,3,2,1,0:T(8,128)} custom-call(f32[8,32,20,40,64]{4,3,2,1,0:T(8,128)} %last.5.refs_0_, f32[2,4,2,800,256]{4,3,2,1,0:T(8,128)} %get-tuple-element.33.refs_1_, f32[8,4,40,384]{3,2,1,0:T(8,128)} %bitcast.34, bf16[160,976]{1,0:T(8,128)(2,1)} %copy-done.7, ...), custom_call_target="tpu_custom_call", output_to_operand_aliasing={{}: (0, {})} | custom-call | flops 960000000 | bytes 27262976 | tf_op jit(solution)/shard_map/last/pallas_call | solution.py:400
  374.3 27.7 %last.7 = f32[8,32,20,40,64]{4,3,2,1,0:T(8,128)} custom-call(f32[8,32,20,40,64]{4,3,2,1,0:T(8,128)} %last.6.refs_0_, f32[2,4,2,800,256]{4,3,2,1,0:T(8,128)} %get-tuple-element.34.refs_1_, f32[8,4,40,384]{3,2,1,0:T(8,128)} %bitcast.35, bf16[160,976]{1,0:T(8,128)(2,1)} %copy-done.7, ...), custom_call_target="tpu_custom_call", output_to_operand_aliasing={{}: (0, {})} | custom-call | flops 960000000 | bytes 27262976 | tf_op jit(solution)/shard_map/last/pallas_call | solution.py:400
  (62 shorter events, 11.6 us)
Async XLA Ops:
  6.5 72.9 %reduce-scatter.5.cloned.1.call-start = ((), (), s32[]{:S(2)}) async-start(), calls=%async_computation.4 | async-start | bytes 2211840 | tf_op jit(solution)/shard_map/reduce_scatter | solution.py:456
  12.3 33.1 %copy-start.16 = (f32[2,20,20]{2,0,1:T(2,128)S(1)}, f32[2,20,20]{2,0,1:T(2,128)}, u32[]{:S(2)}) copy-start(f32[2,20,20]{2,0,1:T(2,128)} %param.20) | copy-start | bytes 9604
  12.3 33.1 %copy-start.17 = (f32[2,20]{1,0:T(2,128)S(1)}, f32[2,20]{1,0:T(2,128)}, u32[]{:S(2)}) copy-start(f32[2,20]{1,0:T(2,128)} %param.21) | copy-start | bytes 484
  44.8 60.2 %all-gather.9.cloned.1.call-start = ((), (), s32[]{:S(2)}) async-start(), calls=%async_computation.8 | async-start | bytes 2211840 | tf_op jit(solution)/shard_map/all_gather | solution.py:459
  45.5 18.0 %copy-start.15 = (f32[2,256,64]{2,1,0:T(8,128)S(1)}, f32[2,256,64]{2,1,0:T(8,128)}, u32[]{:S(2)}) copy-start(f32[2,256,64]{2,1,0:T(8,128)} %constant.56.clone) | copy-start | bytes 393220
  45.6 18.0 %copy-start.8 = (f32[2,256,16]{2,1,0:T(8,128)S(1)}, f32[2,256,16]{2,1,0:T(8,128)}, u32[]{:S(2)}) copy-start(f32[2,256,16]{2,1,0:T(8,128)} %constant.57.clone.refs_1_) | copy-start | bytes 98308
  45.6 18.0 %copy-start.13 = (bf16[3,20,976]{2,1,0:T(8,128)(2,1)S(1)}, bf16[3,20,976]{2,1,0:T(8,128)(2,1)}, u32[]{:S(2)}) copy-start(bf16[3,20,976]{2,1,0:T(8,128)(2,1)} %constant.59.clone.refs_6_) | copy-start | bytes 351364
  45.6 18.0 %copy-start.14 = (bf16[160,20]{1,0:T(8,128)(2,1)S(1)}, bf16[160,20]{1,0:T(8,128)(2,1)}, u32[]{:S(2)}) copy-start(bf16[160,20]{1,0:T(8,128)(2,1)} %constant.58.clone.refs_5_) | copy-start | bytes 19204
  63.6 1.5 copy-start.1
  67.1 2.0 copy-start
  69.8 9.7 %copy-start.4 = (bf16[160,976]{1,0:T(8,128)(2,1)}, bf16[160,976]{1,0:T(8,128)(2,1)S(1)}, u32[]{:S(2)}) copy-start(bf16[160,976]{1,0:T(8,128)(2,1)S(1)} %get-tuple-element.20.refs_0_.refs_4_.refs_5_) | copy-start | bytes 936964
  69.8 9.7 %copy-start.5 = (bf16[512,384]{1,0:T(8,128)(2,1)S(1)}, bf16[512,384]{1,0:T(8,128)(2,1)}, u32[]{:S(2)}) copy-start(bf16[512,384]{1,0:T(8,128)(2,1)} %constant.55.clone.refs_5_) | copy-start | bytes 1179652
  69.8 9.7 %copy-start.6 = (bf16[384,512]{1,0:T(8,128)(2,1)S(1)}, bf16[384,512]{1,0:T(8,128)(2,1)}, u32[]{:S(2)}) copy-start(bf16[384,512]{1,0:T(8,128)(2,1)} %constant.54.clone.refs_4_) | copy-start | bytes 1179652
  79.4 0.9 copy-start.10
  82.7 64.4 %reduce-scatter.7.cloned.1.call-start = ((), (), s32[]{:S(2)}) async-start(), calls=%async_computation.5 | async-start | bytes 2211840 | tf_op jit(solution)/shard_map/reduce_scatter | solution.py:456
  100.6 93.9 %all-gather.11.cloned.1.call-start = ((), (), s32[]{:S(2)}) async-start(), calls=%async_computation.9 | async-start | bytes 2211840 | tf_op jit(solution)/shard_map/all_gather | solution.py:459
  147.1 1.5 copy-start.3
  148.7 0.9 copy-start.11
  151.9 84.8 %reduce-scatter.9.cloned.1.call-start = ((), (), s32[]{:S(2)}) async-start(), calls=%async_computation.6 | async-start | bytes 2211840 | tf_op jit(solution)/shard_map/reduce_scatter | solution.py:456
  194.2 89.8 %all-gather.13.cloned.1.call-start = ((), (), s32[]{:S(2)}) async-start(), calls=%async_computation.10 | async-start | bytes 2211840 | tf_op jit(solution)/shard_map/all_gather | solution.py:459
  236.7 1.5 copy-start.2
  238.2 0.9 copy-start.12
  241.4 74.1 %reduce-scatter.11.cloned.1.call-start = ((), (), s32[]{:S(2)}) async-start(), calls=%async_computation.7 | async-start | bytes 2211840 | tf_op jit(solution)/shard_map/reduce_scatter | solution.py:456
  283.8 62.8 %all-gather.15.cloned.1.call-start = ((), (), s32[]{:S(2)}) async-start(), calls=%async_computation.11 | async-start | bytes 2211840 | tf_op jit(solution)/shard_map/all_gather | solution.py:459
  (2 other events, 1.7 us)
Sparse Core Ops, SparseCore 0:
  45.0 34.4 reduce-scatter.4
  82.8 22.1 all-gather.8
  108.4 31.6 reduce-scatter.6
  152.0 21.3 all-gather.10
  194.4 31.6 reduce-scatter.8
  241.6 21.3 all-gather.12
  283.9 31.6 reduce-scatter.10
  318.9 21.3 all-gather.14

commit v4 on v3

--- a/solution.py
+++ b/solution.py
@@ -376,6 +376,7 @@
 
         native = jnp.transpose(field, (0, 1, 4, 3, 2))
         xy_spec = full(xy.shape)
+        packed_at = lambda at: pl.BlockSpec((1, 1, 2, width * grid_z, LANES), lambda b, g: (at + b, g, 0, 0, 0))
         packed_block = pl.BlockSpec((1, 1, 2, width * grid_z, LANES), lambda b, g: (b, g, 0, 0, 0))
         rows_scr = pltpu.VMEM((width, trigs, PACK), F32)
         zs_scr = pltpu.VMEM((rows, LANES), F32)
@@ -413,15 +414,15 @@
                 input_output_aliases={} if into is None else {0: 0},
                 compiler_params=params(56), cost_estimate=cost(8, n), name='forward')
 
-        def middle(first, n, at, coef, into, after):
+        def middle(first, n, at, coef, into, into_v, size_v, after):
             return ordered(
-                functools.partial(middle_kernel, width, trigs, grid_z), after if into is None else [into] + after,
+                functools.partial(middle_kernel, width, trigs, grid_z), [a for a in (into, into_v) if a is not None] + after,
                 field_blocks(first) + [sums_block(at), full(mix[0].shape), full(z_inv.shape), full(z_fwd.shape), xy_spec, full(xyt.shape), full(pq.shape)],
                 [native, native, coef, mix[0], z_inv, z_fwd, xy, xyt, pq],
-                grid=(n, groups), out_specs=[packed_block, sums_block(at)],
-                out_shape=[jax.ShapeDtypeStruct((n, groups, 2, width * grid_z, LANES), F32), sums],
+                grid=(n, groups), out_specs=[packed_block if into_v is None else packed_at(at), sums_block(at)],
+                out_shape=[jax.ShapeDtypeStruct((size_v, groups, 2, width * grid_z, LANES), F32), sums],
                 scratch_shapes=[rows_scr, gs_scr, sp_scr, u_scr, zs_scr, ts_scr, acc_scr],
-                input_output_aliases={} if into is None else {0: 1},
+                input_output_aliases={} if into is None else {0: 1} if into_v is None else {0: 1, 1: 0},
                 compiler_params=params(60), cost_estimate=cost(20, n), name='middle')
 
         def last(first, n, at, v, coef, out, after):
@@ -465,22 +466,21 @@
         coef_a = spread(mix_a)
         fwd_b = forward(half + part, part, part, fwd_b, [mix_a])
         sum_b = gather_sum(fwd_b)
-        v_0, mid_a = middle(0, part, 0, coef_a, None, [fwd_b])
+        v_0, mid_a = middle(0, part, 0, coef_a, None, None, part, [fwd_b])
         mix_b = mixing(sum_b, 0, [mid_a])
         coef_b = spread(mix_b)
-        v_1, mid_a = middle(part, part, part, coef_a, mid_a, [mix_b])
+        v_1, mid_a = middle(part, part, part, coef_a, mid_a, None, part, [mix_b])
         sum_a = gather_sum(mid_a)
-        v_2, mid_b = middle(half, part, 0, coef_b, None, [mid_a])
+        v_b, mid_b = middle(half, part, 0, coef_b, None, None, half, [mid_a])
         mix_a = mixing(sum_a, 1, [mid_b])
         coef_a = spread(mix_a)
-        v_3, mid_b = middle(half + part, part, part, coef_b, mid_b, [mix_a])
+        v_b, mid_b = middle(half + part, part, part, coef_b, mid_b, v_b, half, [mix_a])
         sum_b = gather_sum(mid_b)
         out = last(0, part, 0, v_0, coef_a, None, [mid_b])
         mix_b = mixing(sum_b, 1, [out])
         coef_b = spread(mix_b)
         out = last(part, part, part, v_1, coef_a, out, [mix_b])
-        out = last(half, part, 0, v_2, coef_b, out, [])
-        out = last(half + part, part, part, v_3, coef_b, out, [])
+        out = last(half, half, 0, v_b, coef_b, out, [])
         return jnp.transpose(out, (0, 1, 4, 3, 2))
 
     field_spec = P('data', 'xs', 'ys', None, None)

time: 412 us -> 406 us (0.985)
  Pallas kernels: 366 us -> 361 us
    pallas_call x16 -> x15, Pallas kernels: 359 us -> 353 us  [ordered(): pl.pallas_call(lambda *refs: kernel(*refs[extra:]), in_specs=[pl.BlockSpe...]
  transfers between devices with their start and end apart: 8 -> 8, of which waited for: 3 -> 3; matrix products, arithmetic and copies ran while one was open for 0% -> 0% of each run, Pallas kernels for 66% -> 67%
where the time goes in v4:
time: 406 us; the launch traced here: 403 us
  Pallas kernels  361 us (89%)
  local copies, waits for them, and re-layouts  14.3 us (4%)
  between operations  13.9 us (3%)
  waiting for transfers between devices  10.2 us (3%)
    pallas_call x15, Pallas kernels, ordered(): pl.pallas_call(lambda *refs: kernel(*refs[extra:]), in_specs=[pl.BlockSpe...  353 us
    unnamed x37, local copies, waits for them, and re-layouts  11.1 us
  transfers between devices with their start and end apart: 8, of which 3 were waited for; matrix products, arithmetic and copies ran while one was open for 0% of the time, Pallas kernels for 67%

profile of v4, /device:TPU:0, one launch (start us, length us, event | category | flops | bytes accessed | tf_op | source)
XLA Modules:
  0.0 403.4 jit_solution(1447122642392954104)
XLA Ops:
  10.3 2.0 pad_maximum_fusion.refs_3_.refs_5_.refs_7_.refs_8_.refs_9_
  12.3 32.5 %forward.4 = f32[8,4,40,384]{3,2,1,0:T(8,128)} custom-call(f32[8,32,20,40,64]{4,3,2,1,0:T(8,128)} %bitcast.refs_0_.refs_1_.refs_2_.refs_3_.refs_4_, f32[8,32,20,40,64]{4,3,2,1,0:T(8,128)} %bitcast.refs_0_.refs_1_.refs_2_.refs_3_.refs_4_, bf16[96,240]{1,0:T(8,128)(2,1)} %constant.52.clone.refs_2_.refs_4_.refs_6_.refs_7_.refs_8_, ...), custom_call_target="tpu_custom_call" | custom-call | flops 1280000000 | bytes 54525952 | tf_op jit(solution)/shard_map/forward/pallas_call | solution.py:401
  45.6 17.9 %forward.3.refs_0_ = f32[8,4,40,384]{3,2,1,0:T(8,128)} custom-call(f32[8,32,20,40,64]{4,3,2,1,0:T(8,128)} %bitcast.refs_0_.refs_1_.refs_2_.refs_3_.refs_4_, f32[8,32,20,40,64]{4,3,2,1,0:T(8,128)} %bitcast.refs_0_.refs_1_.refs_2_.refs_3_.refs_4_, bf16[96,240]{1,0:T(8,128)(2,1)} %constant.52.clone.refs_2_.refs_4_.refs_6_.refs_7_.refs_8_, ...), custom_call_target="tpu_custom_call" | custom-call | flops 640000000 | bytes 27262976 | tf_op jit(solution)/shard_map/forward/pallas_call | solution.py:401
  63.6 1.5 copy-done.1
  65.1 1.9 tables.1
  67.1 2.0 copy-done
  69.8 7.6 %weights.1 = (f32[20,20,256]{2,1,0:T(8,128)S(1)}, f32[20,20,256]{2,1,0:T(8,128)S(1)}, f32[20,20,256]{2,1,0:T(8,128)S(1)}, f32[20,20,256]{2,1,0:T(8,128)S(1)}) custom-call(f32[10240,8,1,20]{3,2,1,0:T(1,128)} %bitcast.29, f32[10240,8,1,20]{3,2,1,0:T(1,128)} %bitcast.30), custom_call_target="tpu_custom_call" | custom-call | flops 400000000 | bytes 16777216 | tf_op jit(solution)/shard_map/weights/pallas_call | solution.py:370
  77.3 2.1 reduce-scatter.5.cloned.1.call-done
  80.4 2.3 mixing.4.refs_1_
  82.8 17.9 %forward.5.refs_0_ = f32[8,4,40,384]{3,2,1,0:T(8,128)} custom-call(f32[8,4,40,384]{3,2,1,0:T(8,128)} %forward.3.refs_0_, f32[4,40,384]{2,1,0:T(8,128)} %mixing.4.refs_1_, f32[8,32,20,40,64]{4,3,2,1,0:T(8,128)} %bitcast.refs_0_.refs_1_.refs_2_.refs_3_.refs_4_, ...), custom_call_target="tpu_custom_call", output_to_operand_aliasing={{}: (0, {})} | custom-call | flops 640000000 | bytes 27262976 | tf_op jit(solution)/shard_map/forward/pallas_call | solution.py:401
  100.9 4.1 %all-gather.9.cloned.1.call-done = f32[32,40,384]{2,1,0:T(8,128)} async-done(((f32[4,40,384]{2,1,0:T(8,128)}), f32[32,40,384]{2,1,0:T(8,128)}) %all-gather.9.cloned.1.call-update) | async-done | bytes 1966096 | tf_op jit(solution)/shard_map/all_gather | solution.py:460
  105.0 42.0 %middle.4 = (f32[2,4,2,800,256]{4,3,2,1,0:T(8,128)}, f32[8,4,40,384]{3,2,1,0:T(8,128)}) custom-call(f32[8,4,40,384]{3,2,1,0:T(8,128)} %forward.5.refs_0_, f32[8,32,20,40,64]{4,3,2,1,0:T(8,128)} %bitcast.refs_0_.refs_1_.refs_2_.refs_3_.refs_4_, f32[8,32,20,40,64]{4,3,2,1,0:T(8,128)} %bitcast.refs_0_.refs_1_.refs_2_.refs_3_.refs_4_, ...), custom_call_target="tpu_custom_call" | custom-call | flops 1600000000 | bytes 27262976 | tf_op jit(solution)/shard_map/middle/pallas_call | solution.py:401
  147.1 1.5 copy-done.3
  149.6 2.3 mixing.5.refs_1_
  151.9 42.2 %middle.5 = (f32[2,4,2,800,256]{4,3,2,1,0:T(8,128)}, f32[8,4,40,384]{3,2,1,0:T(8,128)}) custom-call(f32[8,4,40,384]{3,2,1,0:T(8,128)} %get-tuple-element.24.refs_0_, f32[4,40,384]{2,1,0:T(8,128)} %mixing.5.refs_1_, f32[8,32,20,40,64]{4,3,2,1,0:T(8,128)} %bitcast.refs_0_.refs_1_.refs_2_.refs_3_.refs_4_, ...), custom_call_target="tpu_custom_call", output_to_operand_aliasing={{1}: (0, {})} | custom-call | flops 1600000000 | bytes 27262976 | tf_op jit(solution)/shard_map/middle/pallas_call | solution.py:401
  194.4 42.2 %middle.6 = (f32[4,4,2,800,256]{4,3,2,1,0:T(8,128)}, f32[8,4,40,384]{3,2,1,0:T(8,128)}) custom-call(f32[8,4,40,384]{3,2,1,0:T(8,128)} %get-tuple-element.25.refs_0_, f32[8,32,20,40,64]{4,3,2,1,0:T(8,128)} %bitcast.refs_0_.refs_1_.refs_2_.refs_3_.refs_4_, f32[8,32,20,40,64]{4,3,2,1,0:T(8,128)} %bitcast.refs_0_.refs_1_.refs_2_.refs_3_.refs_4_, ...), custom_call_target="tpu_custom_call" | custom-call | flops 1600000000 | bytes 27262976 | tf_op jit(solution)/shard_map/middle/pallas_call | solution.py:401
  236.6 1.5 copy-done.2
  239.1 2.3 mixing.6.refs_2_
  241.5 42.2 %middle.7 = (f32[4,4,2,800,256]{4,3,2,1,0:T(8,128)}, f32[8,4,40,384]{3,2,1,0:T(8,128)}) custom-call(f32[8,4,40,384]{3,2,1,0:T(8,128)} %get-tuple-element.26.refs_0_, f32[4,4,2,800,256]{4,3,2,1,0:T(8,128)} %get-tuple-element.27.refs_1_, f32[4,40,384]{2,1,0:T(8,128)} %mixing.6.refs_2_, ...), custom_call_target="tpu_custom_call", output_to_operand_aliasing={{1}: (0, {}), {0}: (1, {})} | custom-call | flops 1600000000 | bytes 27262976 | tf_op jit(solution)/shard_map/middle/pallas_call | solution.py:401
  284.0 27.7 %last.3.refs_0_ = f32[8,32,20,40,64]{4,3,2,1,0:T(8,128)} custom-call(f32[8,4,40,384]{3,2,1,0:T(8,128)} %get-tuple-element.30.refs_0_, f32[2,4,2,800,256]{4,3,2,1,0:T(8,128)} %get-tuple-element.31.refs_1_, f32[8,4,40,384]{3,2,1,0:T(8,128)} %bitcast.32, bf16[160,976]{1,0:T(8,128)(2,1)} %copy-done.7, ...), custom_call_target="tpu_custom_call" | custom-call | flops 960000000 | bytes 27262976 | tf_op jit(solution)/shard_map/last/pallas_call | solution.py:401
  311.7 3.8 reduce-scatter.11.cloned.1.call-done
  316.5 2.3 mixing.7.refs_1_
  318.8 27.7 %last.4.refs_0_ = f32[8,32,20,40,64]{4,3,2,1,0:T(8,128)} custom-call(f32[8,32,20,40,64]{4,3,2,1,0:T(8,128)} %last.3.refs_0_, f32[4,40,384]{2,1,0:T(8,128)} %mixing.7.refs_1_, f32[2,4,2,800,256]{4,3,2,1,0:T(8,128)} %get-tuple-element.33.refs_2_, f32[8,4,40,384]{3,2,1,0:T(8,128)} %bitcast.33, ...), custom_call_target="tpu_custom_call", output_to_operand_aliasing={{}: (0, {})} | custom-call | flops 960000000 | bytes 27262976 | tf_op jit(solution)/shard_map/last/pallas_call | solution.py:401
  346.5 49.8 %last.5 = f32[8,32,20,40,64]{4,3,2,1,0:T(8,128)} custom-call(f32[8,32,20,40,64]{4,3,2,1,0:T(8,128)} %last.4.refs_0_, f32[4,4,2,800,256]{4,3,2,1,0:T(8,128)} %get-tuple-element.34.refs_1_, f32[8,4,40,384]{3,2,1,0:T(8,128)} %bitcast.39, bf16[160,976]{1,0:T(8,128)(2,1)} %copy-done.7, ...), custom_call_target="tpu_custom_call", output_to_operand_aliasing={{}: (0, {})} | custom-call | flops 1920000000 | bytes 54525952 | tf_op jit(solution)/shard_map/last/pallas_call | solution.py:401
  (61 shorter events, 10.0 us)
Async XLA Ops:
  6.5 72.9 %reduce-scatter.5.cloned.1.call-start = ((), (), s32[]{:S(2)}) async-start(), calls=%async_computation.4 | async-start | bytes 2211840 | tf_op jit(solution)/shard_map/reduce_scatter | solution.py:457
  12.3 33.1 %copy-start.16 = (f32[2,20,20]{2,0,1:T(2,128)S(1)}, f32[2,20,20]{2,0,1:T(2,128)}, u32[]{:S(2)}) copy-start(f32[2,20,20]{2,0,1:T(2,128)} %param.20) | copy-start | bytes 9604
  12.3 33.1 %copy-start.17 = (f32[2,20]{1,0:T(2,128)S(1)}, f32[2,20]{1,0:T(2,128)}, u32[]{:S(2)}) copy-start(f32[2,20]{1,0:T(2,128)} %param.21) | copy-start | bytes 484
  44.8 60.2 %all-gather.9.cloned.1.call-start = ((), (), s32[]{:S(2)}) async-start(), calls=%async_computation.8 | async-start | bytes 2211840 | tf_op jit(solution)/shard_map/all_gather | solution.py:460
  45.5 18.0 %copy-start.15 = (f32[2,256,64]{2,1,0:T(8,128)S(1)}, f32[2,256,64]{2,1,0:T(8,128)}, u32[]{:S(2)}) copy-start(f32[2,256,64]{2,1,0:T(8,128)} %constant.56.clone) | copy-start | bytes 393220
  45.5 18.0 %copy-start.8 = (f32[2,256,16]{2,1,0:T(8,128)S(1)}, f32[2,256,16]{2,1,0:T(8,128)}, u32[]{:S(2)}) copy-start(f32[2,256,16]{2,1,0:T(8,128)} %constant.57.clone.refs_1_) | copy-start | bytes 98308
  45.5 18.0 %copy-start.13 = (bf16[3,20,976]{2,1,0:T(8,128)(2,1)S(1)}, bf16[3,20,976]{2,1,0:T(8,128)(2,1)}, u32[]{:S(2)}) copy-start(bf16[3,20,976]{2,1,0:T(8,128)(2,1)} %constant.59.clone.refs_6_) | copy-start | bytes 351364
  45.6 18.0 %copy-start.14 = (bf16[160,20]{1,0:T(8,128)(2,1)S(1)}, bf16[160,20]{1,0:T(8,128)(2,1)}, u32[]{:S(2)}) copy-start(bf16[160,20]{1,0:T(8,128)(2,1)} %constant.58.clone.refs_5_) | copy-start | bytes 19204
  63.6 1.5 copy-start.1
  67.0 2.0 copy-start
  69.7 9.7 %copy-start.4 = (bf16[160,976]{1,0:T(8,128)(2,1)}, bf16[160,976]{1,0:T(8,128)(2,1)S(1)}, u32[]{:S(2)}) copy-start(bf16[160,976]{1,0:T(8,128)(2,1)S(1)} %get-tuple-element.20.refs_0_.refs_4_.refs_5_.refs_6_) | copy-start | bytes 936964
  69.7 9.7 %copy-start.5 = (bf16[512,384]{1,0:T(8,128)(2,1)S(1)}, bf16[512,384]{1,0:T(8,128)(2,1)}, u32[]{:S(2)}) copy-start(bf16[512,384]{1,0:T(8,128)(2,1)} %constant.55.clone.refs_5_) | copy-start | bytes 1179652
  69.8 9.7 %copy-start.6 = (bf16[384,512]{1,0:T(8,128)(2,1)S(1)}, bf16[384,512]{1,0:T(8,128)(2,1)}, u32[]{:S(2)}) copy-start(bf16[384,512]{1,0:T(8,128)(2,1)} %constant.54.clone.refs_4_) | copy-start | bytes 1179652
  79.4 0.9 copy-start.10
  82.7 64.4 %reduce-scatter.7.cloned.1.call-start = ((), (), s32[]{:S(2)}) async-start(), calls=%async_computation.5 | async-start | bytes 2211840 | tf_op jit(solution)/shard_map/reduce_scatter | solution.py:457
  100.7 93.7 %all-gather.11.cloned.1.call-start = ((), (), s32[]{:S(2)}) async-start(), calls=%async_computation.9 | async-start | bytes 2211840 | tf_op jit(solution)/shard_map/all_gather | solution.py:460
  147.1 1.5 copy-start.3
  148.6 0.9 copy-start.11
  151.9 84.8 %reduce-scatter.9.cloned.1.call-start = ((), (), s32[]{:S(2)}) async-start(), calls=%async_computation.6 | async-start | bytes 2211840 | tf_op jit(solution)/shard_map/reduce_scatter | solution.py:457
  194.1 89.9 %all-gather.13.cloned.1.call-start = ((), (), s32[]{:S(2)}) async-start(), calls=%async_computation.10 | async-start | bytes 2211840 | tf_op jit(solution)/shard_map/all_gather | solution.py:460
  236.6 1.5 copy-start.2
  238.2 0.9 copy-start.12
  241.4 74.1 %reduce-scatter.11.cloned.1.call-start = ((), (), s32[]{:S(2)}) async-start(), calls=%async_computation.7 | async-start | bytes 2211840 | tf_op jit(solution)/shard_map/reduce_scatter | solution.py:457
  283.7 62.8 %all-gather.15.cloned.1.call-start = ((), (), s32[]{:S(2)}) async-start(), calls=%async_computation.11 | async-start | bytes 2211840 | tf_op jit(solution)/shard_map/all_gather | solution.py:460
  (2 other events, 1.7 us)
Sparse Core Ops, SparseCore 0:
  44.9 34.4 reduce-scatter.4
  82.8 22.1 all-gather.8
  108.4 31.6 reduce-scatter.6
  152.0 21.3 all-gather.10
  194.2 31.6 reduce-scatter.8
  241.5 21.3 all-gather.12
  283.8 31.6 reduce-scatter.10
  318.9 21.3 all-gather.14
